TPU v7x, 8 devices: a whole 2x2x1 slice. The times are simulated.
8 devices in a mesh: data: 8 (over z, y, x, core).
Axes of the slice: x: 2, y: 2, z: 1, core: 2. Of those that a mesh axis runs over, the one named last changes fastest.
Arguments:
- h_a: bfloat16 [8192, 2048], P('data')
- h_b: bfloat16 [8192, 2048], P('data')
- w_one: bfloat16 [2048, 1024], replicated
- w_two: bfloat16 [1024, 1024], replicated
- w_three: bfloat16 [1024, 1024], replicated
- gain_one: float32 [1024], replicated
- bias_one: float32 [1024], replicated
- gain_two: float32 [1024], replicated
- bias_two: float32 [1024], replicated
Outputs:
- output 1: float32 [], replicated
- output 2: float32 [2048, 1024], replicated
- output 3: float32 [1024, 1024], replicated
- output 4: float32 [1024, 1024], replicated
- output 5: float32 [1024], replicated
- output 6: float32 [1024], replicated
- output 7: float32 [1024], replicated
- output 8: float32 [1024], replicated
All inputs are finite; a program needn't handle non-finite values.
Results may differ from a plain program's by a relative error of at most 0.00107.
Values are sent between devices in bfloat16 or wider.
A program may use at most 1 GiB of HBM per device.

v0:
```python
import jax
import jax.numpy as jnp
from jax import lax
from jax.sharding import PartitionSpec as P

BN_EPS = 1e-5
STD_EPS = 1e-4
INV_WEIGHT = 2.0
VAR_WEIGHT = 1.0
COV_WEIGHT = 2.0


def layer_forward(x_in, weight, gain_vec, bias_vec, all_rows):
    pre_act = jnp.einsum('vnk,kd->vnd', x_in, weight, preferred_element_type=jnp.float32)
    moments = lax.psum(jnp.stack([jnp.sum(pre_act, axis=1), jnp.sum(pre_act * pre_act, axis=1)]), 'data')
    col_mean = moments[0] / all_rows
    col_var = moments[1] / all_rows - col_mean * col_mean
    inv_std = lax.rsqrt(col_var + BN_EPS)[:, None, :]
    normed = (pre_act - col_mean[:, None, :]) * inv_std
    act_val = gain_vec * normed + bias_vec
    return jnp.maximum(act_val, 0.0).astype(jnp.bfloat16), normed, act_val, inv_std


def layer_backward(d_out, normed, act_val, inv_std, gain_vec, all_rows):
    d_act = jnp.where(act_val > 0.0, d_out, 0.0)
    stat_sums = lax.psum(jnp.stack([jnp.sum(d_act, axis=1), jnp.sum(d_act * normed, axis=1)]), 'data')
    d_pre = inv_std * gain_vec * (d_act - stat_sums[0][:, None, :] / all_rows - normed * (stat_sums[1][:, None, :] / all_rows))
    return d_pre.astype(jnp.bfloat16), jnp.sum(stat_sums[1], axis=0), jnp.sum(stat_sums[0], axis=0)


def loss_from_stats(z_views, z_diff, col_sum, gram_mat, sq_sum, all_rows):
    col_mu = col_sum / all_rows
    cov_mat = (gram_mat - all_rows * col_mu[:, :, None] * col_mu[:, None, :]) / (all_rows - 1)
    diag_var = jnp.diagonal(cov_mat, axis1=1, axis2=2)
    std_vec = jnp.sqrt(diag_var + STD_EPS)
    hinge_on = (std_vec < 1.0).astype(jnp.float32)
    loss_val = (INV_WEIGHT * sq_sum / all_rows
                + VAR_WEIGHT * jnp.sum(jnp.maximum(1.0 - std_vec, 0.0))
                + COV_WEIGHT * (jnp.sum(cov_mat * cov_mat) - jnp.sum(diag_var * diag_var)))
    proj_dim = cov_mat.shape[-1]
    eye_mask = lax.broadcasted_iota(jnp.int32, (proj_dim, proj_dim), 0) == lax.broadcasted_iota(jnp.int32, (proj_dim, proj_dim), 1)
    grad_cov = jnp.where(eye_mask, (-VAR_WEIGHT * hinge_on / (2.0 * std_vec))[:, None, :], (2.0 * COV_WEIGHT) * cov_mat)
    g_hat = grad_cov.astype(jnp.bfloat16)
    row_part = jnp.einsum('woe,wef->wof', z_views, g_hat, preferred_element_type=jnp.float32)
    mean_part = jnp.einsum('vd,vde->ve', col_mu, g_hat.astype(jnp.float32), precision=lax.Precision.HIGHEST)
    d_inv = (2.0 * INV_WEIGHT / all_rows) * z_diff
    d_z = ((2.0 / (all_rows - 1)) * (row_part - mean_part[:, None, :]) + jnp.stack([d_inv, -d_inv])).astype(jnp.bfloat16)
    return loss_val, d_z


def solution(mesh):
    group_devs = mesh.shape['data']

    def local_step(h_a, h_b, w_one, w_two, w_three, gain_one, bias_one, gain_two, bias_two):
        all_rows = h_a.shape[0] * group_devs
        view_feats = jnp.stack([h_a, h_b])
        hidden_one, normed_one, act_one, inv_one = layer_forward(view_feats, w_one, gain_one, bias_one, all_rows)
        hidden_two, normed_two, act_two, inv_two = layer_forward(hidden_one, w_two, gain_two, bias_two, all_rows)
        z_views = jnp.einsum('vnk,kd->vnd', hidden_two, w_three, preferred_element_type=jnp.float32).astype(jnp.bfloat16)
        z_diff = z_views[0].astype(jnp.float32) - z_views[1].astype(jnp.float32)
        col_sum, gram_mat, sq_sum = lax.psum(
            (jnp.sum(z_views, axis=1, dtype=jnp.float32),
             jnp.einsum('woe,wof->wef', z_views, z_views, preferred_element_type=jnp.float32),
             jnp.sum(z_diff * z_diff)), 'data')
        loss_val, d_z = loss_from_stats(z_views, z_diff, col_sum, gram_mat, sq_sum, all_rows)
        grad_three = jnp.einsum('vnk,vnd->kd', hidden_two, d_z, preferred_element_type=jnp.float32)
        d_hidden_two = jnp.einsum('vnd,kd->vnk', d_z, w_three, preferred_element_type=jnp.float32)
        d_pre_two, gain_grad_two, bias_grad_two = layer_backward(d_hidden_two, normed_two, act_two, inv_two, gain_two, all_rows)
        grad_two = jnp.einsum('vnk,vnd->kd', hidden_one, d_pre_two, preferred_element_type=jnp.float32)
        d_hidden_one = jnp.einsum('vnd,kd->vnk', d_pre_two, w_two, preferred_element_type=jnp.float32)
        d_pre_one, gain_grad_one, bias_grad_one = layer_backward(d_hidden_one, normed_one, act_one, inv_one, gain_one, all_rows)
        grad_one = jnp.einsum('vnf,vnd->fd', view_feats, d_pre_one, preferred_element_type=jnp.float32)
        grad_one, grad_two, grad_three = lax.psum((grad_one, grad_two, grad_three), 'data')
        return loss_val, grad_one, grad_two, grad_three, gain_grad_one, bias_grad_one, gain_grad_two, bias_grad_two

    row_spec = P('data', None)
    return jax.shard_map(local_step, mesh=mesh,
                         in_specs=(row_spec, row_spec, P(), P(), P(), P(), P(), P(), P()),
                         out_specs=(P(), P(), P(), P(), P(), P(), P(), P()),
                         check_vma=False)
```

profile of v0, /device:TPU:0, one launch (start us, length us, event | category | flops | bytes accessed | tf_op | source)
XLA Modules:
  0.0 603.5 jit_solution(15793410174311509178)
XLA Ops:
  7.2 14.7 %fusion.40 = (f32[2,1024]{1,0:T(2,128)S(1)}, f32[2,1024]{1,0:T(2,128)S(1)}, f32[2,1024,1024]{2,1,0:T(8,128)}) fusion(bf16[2048,1024]{1,0:T(8,128)(2,1)} %param.11, bf16[1,1024,2048]{2,1,0:T(8,128)(2,1)} %bitcast.106, bf16[1,1024,2048]{2,1,0:T(8,128)(2,1)} %bitcast.108), kind=kOutput, calls=%fused_computation.90 | convolution fusion | flops 8600416256 | bytes 20987904 | tf_op jit(solution)/shard_map/vnk,kd->vnd/dot_general | solution.py:14
  21.9 25.2 %psum.70 = f32[2,2,1024]{2,1,0:T(2,128)S(1)} all-reduce(f32[2,2,1024]{2,1,0:T(2,128)S(1)} %pad_maximum_fusion.5), channel_id=1, replica_groups=mesh['data'=8] {'data'}, use_global_device_ids=true, to_apply=%region_2.0 | all-reduce | flops 4096 | bytes 32768 | tf_op jit(solution)/shard_map/psum | solution.py:15
  47.2 10.9 %fusion.39 = (f32[2,1024]{1,0:T(2,128)S(1)}, f32[2,1024]{1,0:T(2,128)S(1)}, f32[2,1024,1024]{2,1,0:T(8,128)}) fusion(bf16[1024,1024]{1,0:T(8,128)(2,1)S(1)} %copy-done, f32[2,1024,1024]{2,1,0:T(8,128)} %get-tuple-element.42, f32[1024]{0:T(1024)S(1)} %copy-done.9, f32[2,1024]{1,0:T(2,128)S(1)} %get-tuple-element.37, f32[2,1024]{1,0:T(2,128)S(1)} %fusion.29, ...), kind=kOutput, calls=%fused_computation.89 | convolution fusion | flops 4313837568 | bytes 18915328 | tf_op jit(solution)/shard_map/vnk,kd->vnd/dot_general | solution.py:14
  58.1 23.7 %psum.71 = f32[2,2,1024]{2,1,0:T(2,128)S(1)} all-reduce(f32[2,2,1024]{2,1,0:T(2,128)S(1)} %pad_maximum_fusion.6), channel_id=1, replica_groups=mesh['data'=8] {'data'}, use_global_device_ids=true, to_apply=%region_5.0 | all-reduce | flops 4096 | bytes 32768 | tf_op jit(solution)/shard_map/psum | solution.py:15
  81.9 8.7 %convert_reduce_fusion = (f32[2,1024]{1,0:T(2,128)S(1)}, bf16[2,1024,1024]{2,1,0:T(8,128)(2,1)S(1)}) fusion(bf16[1024,1024]{1,0:T(8,128)(2,1)} %param.13, f32[2,1024,1024]{2,1,0:T(8,128)} %get-tuple-element.43, f32[1024]{0:T(1024)S(1)} %copy-done.8, f32[2,1024]{1,0:T(2,128)S(1)} %get-tuple-element.39, f32[2,1024]{1,0:T(2,128)S(1)} %fusion.23, ...), kind=kOutput, calls=%fused_computation.11 | convolution fusion | flops 4313839616 | bytes 14712832 | tf_op jit(solution)/shard_map/vnk,kd->vnd/dot_general | solution.py:59
  90.6 2.0 copy-done.3
  92.6 6.8 %fusion.42 = f32[2,1024,1024]{2,1,0:T(8,128)} fusion(bf16[2,1024,1024]{2,1,0:T(8,128)(2,1)S(1)} %get-tuple-element.45), kind=kOutput, calls=%fused_computation.91 | convolution fusion | flops 4294967296 | bytes 12582912 | tf_op jit(solution)/shard_map/woe,wof->wef/dot_general | solution.py:63
  99.5 25.0 %psum.74 = f32[2,1024]{1,0:T(2,128)S(1)} all-reduce(f32[2,1024]{1,0:T(2,128)S(1)} %get-tuple-element.44), channel_id=1, replica_groups=mesh['data'=8] {'data'}, use_global_device_ids=true, to_apply=%region_10.0 | all-reduce | flops 2048 | bytes 16384 | tf_op jit(solution)/shard_map/psum | solution.py:61
  124.5 0.3 iota_compare_fusion
  124.8 7.5 %fusion.11 = (f32[1,1024,1024]{2,1,0:T(8,128)}, f32[1,1024,1024]{2,1,0:T(8,128)}, f32[]{:T(128)}) fusion(bf16[2,1024,1024]{2,1,0:T(8,128)(2,1)} %copy-done.3), kind=kLoop, calls=%fused_computation.35 | loop fusion | flops 7340031 | bytes 12582916 | tf_op jit(solution)/shard_map/mul | solution.py:46
  132.3 84.9 %all-reduce.5.cloned.1.call-done = f32[2,1024,1024]{2,1,0:T(8,128)} async-done(((f32[2,1024,1024]{2,1,0:T(8,128)}), f32[2,1024,1024]{2,1,0:T(8,128)}) %all-reduce.5.cloned.1.call-update) | async-done | bytes 8388624 | tf_op jit(solution)/shard_map/psum | solution.py:61
  217.2 5.8 multiply_reduce_fusion.2
  223.1 12.9 %copy.23 = f32[2,1024,1024]{2,0,1:T(2,128)} copy(f32[2,1024,1024]{2,1,0:T(8,128)S(1)} %get-tuple-element.28) | data formatting | bytes 16777216 | tf_op jit(solution)/shard_map/div | solution.py:33
  236.0 12.3 %gather_fusion = f32[1024,2]{0,1:T(2,128)S(1)} fusion(f32[2,1024,1024]{2,0,1:T(2,128)} %copy.23, s32[1024]{0:T(1024)S(1)} %bitcast.94), kind=kCustom, calls=%fused_computation | custom fusion | bytes 24576 | tf_op jit(solution)/shard_map/jit(diagonal)/gather | solution.py:34
  248.3 5.7 fusion.30
  254.0 10.3 %fusion = bf16[2,1024,1024]{2,1,0:T(8,128)(2,1)} fusion(f32[1,1024,1024]{2,1,0:T(8,128)} %get-tuple-element.30, f32[1,1024,1024]{2,1,0:T(8,128)} %get-tuple-element.29, f32[2,1024]{1,0:T(2,128)S(1)} %bitcast.97, bf16[2,1024,1024]{2,1,0:T(8,128)(2,1)S(1)} %copy-done.4, f32[2,1024,1024]{2,1,0:T(8,128)} %all-reduce.5.cloned.1.call-done, ...), kind=kOutput, calls=%fused_computation.3 | convolution fusion | flops 4313841664 | bytes 26243072 | tf_op jit(solution)/shard_map/woe,wef->wof/dot_general | solution.py:44
  264.4 8.8 %convolution_bitcast_fusion = f32[1024,1024]{1,0:T(8,128)} fusion(bf16[2,1024,1024]{2,1,0:T(8,128)(2,1)} %fusion, f32[2,1024,1024]{2,1,0:T(8,128)S(1)} %bitcast.96, f32[1024]{0:T(1024)S(1)} %copy-done.8, f32[2,1024]{1,0:T(2,128)S(1)} %get-tuple-element.39, f32[2,1024]{1,0:T(2,128)S(1)} %fusion.23, f32[1024]{0:T(1024)S(1)} %copy-done.5), kind=kOutput, calls=%fused_computation.37 | convolution fusion | flops 4307550208 | bytes 16801792 | tf_op jit(solution)/shard_map/vnk,vnd->kd/dot_general | solution.py:66
  273.2 8.8 %fusion.38 = (f32[2,1024]{1,0:T(2,128)S(1)}, f32[2,1024]{1,0:T(2,128)S(1)}, f32[2,1024,1024]{2,1,0:T(8,128)}) fusion(f32[2,1024]{1,0:T(2,128)S(1)} %get-tuple-element.39, f32[2,1024,1024]{2,1,0:T(8,128)S(1)} %bitcast.96, f32[2,1024]{1,0:T(2,128)S(1)} %fusion.23, bf16[2,1024,1024]{2,1,0:T(8,128)(2,1)S(1)} %copy-done.10, ...), kind=kOutput, calls=%fused_computation.88 | convolution fusion | flops 4313837568 | bytes 23109632 | tf_op jit(solution)/shard_map/vnd,kd->vnk/dot_general | solution.py:67
  282.0 22.7 %psum.75 = f32[2,2,1024]{2,1,0:T(2,128)S(1)} all-reduce(f32[2,2,1024]{2,1,0:T(2,128)S(1)} %pad_maximum_fusion.7), channel_id=1, replica_groups=mesh['data'=8] {'data'}, use_global_device_ids=true, to_apply=%region_16.17 | all-reduce | flops 4096 | bytes 32768 | tf_op jit(solution)/shard_map/psum | solution.py:26
  304.7 0.6 slice_reduce_fusion.3
  305.3 7.2 %multiply_convert_fusion.1 = bf16[2,1024,1024]{2,1,0:T(8,128)(2,1)S(1)} fusion(f32[2,1024,1024]{2,1,0:T(8,128)} %get-tuple-element.46, f32[2,1024,1024]{2,1,0:T(8,128)} %get-tuple-element.43, f32[2,1024]{1,0:T(2,128)S(1)} %get-tuple-element.32, f32[2,1024]{1,0:T(2,128)S(1)} %get-tuple-element.33, f32[2,1024]{1,0:T(2,128)S(1)} %get-tuple-element.38, ...), kind=kLoop, calls=%fused_computation.6 | loop fusion | flops 14680064 | bytes 21012480 | tf_op jit(solution)/shard_map/convert_element_type | solution.py:28
  312.5 9.7 %convolution_bitcast_fusion.1 = f32[1024,1024]{1,0:T(8,128)} fusion(bf16[2,1024,1024]{2,1,0:T(8,128)(2,1)S(1)} %multiply_convert_fusion.1, f32[2,1024,1024]{2,1,0:T(8,128)} %get-tuple-element.42, f32[1024]{0:T(1024)S(1)} %copy-done.9, f32[2,1024]{1,0:T(2,128)S(1)} %get-tuple-element.37, f32[2,1024]{1,0:T(2,128)S(1)} %fusion.29, f32[1024]{0:T(1024)S(1)} %copy-done.6), kind=kOutput, calls=%fused_computation.38 | convolution fusion | flops 4307550208 | bytes 16801792 | tf_op jit(solution)/shard_map/vnk,vnd->kd/dot_general | solution.py:69
  322.2 8.6 %fusion.37 = (f32[2,1024]{1,0:T(2,128)S(1)}, f32[2,1024]{1,0:T(2,128)S(1)}, f32[2,1024,1024]{2,1,0:T(8,128)}) fusion(f32[2,1024]{1,0:T(2,128)S(1)} %get-tuple-element.37, f32[2,1024,1024]{2,1,0:T(8,128)S(1)} %bitcast.111, f32[2,1024]{1,0:T(2,128)S(1)} %fusion.29, bf16[2,1024,1024]{2,1,0:T(8,128)(2,1)S(1)} %multiply_convert_fusion.1, ...), kind=kOutput, calls=%fused_computation.87 | convolution fusion | flops 4313837568 | bytes 23109632 | tf_op jit(solution)/shard_map/vnd,kd->vnk/dot_general | solution.py:70
  330.9 24.6 %all-reduce = (f32[]{:T(128)}, f32[2,2,1024]{2,1,0:T(2,128)S(1)}) all-reduce(f32[]{:T(128)} %get-tuple-element.31, f32[2,2,1024]{2,1,0:T(2,128)S(1)} %pad_maximum_fusion.8), channel_id=1, replica_groups=mesh['data'=8] {'data'}, use_global_device_ids=true, to_apply=%region_7.0 | all-reduce | flops 4097 | bytes 32776 | tf_op jit(solution)/shard_map/psum | solution.py:61
  355.5 0.6 slice_reduce_fusion.1
  356.1 17.4 %fusion.4 = f32[2048,1024]{1,0:T(8,128)} fusion(bf16[1,1024,2048]{2,1,0:T(8,128)(2,1)} %bitcast.107, bf16[1,1024,2048]{2,1,0:T(8,128)(2,1)} %bitcast.109, f32[2,1024,1024]{2,1,0:T(8,128)} %get-tuple-element.47, f32[2,1024,1024]{2,1,0:T(8,128)} %get-tuple-element.42, f32[2,1024]{1,0:T(2,128)S(1)} %get-tuple-element.34, f32[2,1024]{1,0:T(2,128)S(1)} %get-tuple-element.35, ...), kind=kOutput, calls=%fused_computation.25 | convolution fusion | flops 8608808960 | bytes 33595392 | tf_op jit(solution)/shard_map/vnf,vnd->fd/dot_general | solution.py:72
  373.5 0.6 multiply_reduce_fusion.6
  376.7 204.0 %all-reduce.7.cloned.1.call-done = (f32[2048,1024]{1,0:T(8,128)}, f32[1024,1024]{1,0:T(8,128)}, f32[1024,1024]{1,0:T(8,128)}) async-done(((f32[2048,1024]{1,0:T(8,128)}, f32[1024,1024]{1,0:T(8,128)}, f32[1024,1024]{1,0:T(8,128)}), (f32[2048,1024]{1,0:T(8,128)}, f32[1024,1024]{1,0:T(8,128)}, f32[1024,1024]{1,0:T(8,128)})) %all-reduce.7.cloned.1.call-update) | async-done | bytes 16777232 | tf_op jit(solution)/shard_map/psum | solution.py:73
  580.7 8.6 %copy.41 = f32[2048,1024]{1,0:T(8,128)} copy(f32[2048,1024]{1,0:T(8,128)} %get-tuple-element.49) | data formatting | bytes 16777216
  589.3 2.1 copy.42
  591.4 1.6 copy-done.1
  593.0 2.0 copy.43
  (46 shorter events, 0.3 us)
Async XLA Ops:
  7.2 40.0 %copy-start = (bf16[1024,1024]{1,0:T(8,128)(2,1)S(1)}, bf16[1024,1024]{1,0:T(8,128)(2,1)}, u32[]{:S(2)}) copy-start(bf16[1024,1024]{1,0:T(8,128)(2,1)} %param.12) | copy-start | bytes 6291460
  7.2 210.0 %all-reduce.5.cloned.1.call-start = ((), (), s32[]{:S(2)}) async-start(), calls=%async_computation | async-start | bytes 16777216 | tf_op jit(solution)/shard_map/psum | solution.py:61
  7.2 39.9 %copy-start.6 = (f32[1024]{0:T(1024)S(1)}, f32[1024]{0:T(1024)}, u32[]{:S(2)}) copy-start(f32[1024]{0:T(1024)} %param.14) | copy-start | bytes 12292
  7.2 39.9 %copy-start.9 = (f32[1024]{0:T(1024)S(1)}, f32[1024]{0:T(1024)}, u32[]{:S(2)}) copy-start(f32[1024]{0:T(1024)} %param.15) | copy-start | bytes 12292
  47.2 34.7 %copy-start.5 = (f32[1024]{0:T(1024)S(1)}, f32[1024]{0:T(1024)}, u32[]{:S(2)}) copy-start(f32[1024]{0:T(1024)} %param.16) | copy-start | bytes 12292
  47.2 34.7 %copy-start.8 = (f32[1024]{0:T(1024)S(1)}, f32[1024]{0:T(1024)}, u32[]{:S(2)}) copy-start(f32[1024]{0:T(1024)} %param.17) | copy-start | bytes 12292
  90.6 2.0 copy-start.3
  99.4 481.3 %all-reduce.7.cloned.1.call-start = ((), (), s32[]{:S(2)}) async-start(), calls=%async_computation.1 | async-start | bytes 33554432 | tf_op jit(solution)/shard_map/psum | solution.py:73
  248.2 5.8 copy-start.4
  248.3 16.1 %slice-start = ((s8[8388608]{0:T(1024)(128)(4,1)}), s8[4194304]{0:T(1024)(128)(4,1)S(1)}, s32[]{:S(2)}) async-start(s8[8388608]{0:T(1024)(128)(4,1)} %bitcast.95), calls=%async_computation.2 | async-start | bytes 8388608
  254.0 10.3 %slice-start.1 = ((s8[8388608]{0:T(1024)(128)(4,1)}), s8[4194304]{0:T(1024)(128)(4,1)S(1)}, s32[]{:S(2)}) async-start(s8[8388608]{0:T(1024)(128)(4,1)} %bitcast.95), calls=%async_computation.3 | async-start | bytes 8388608
  264.4 8.9 %copy-start.7 = (bf16[1024,1024]{1,0:T(8,128)(2,1)S(1)}, bf16[1024,1024]{1,0:T(8,128)(2,1)}, u32[]{:S(2)}) copy-start(bf16[1024,1024]{1,0:T(8,128)(2,1)} %param.13) | copy-start | bytes 6291460
  264.4 8.8 %copy-start.10 = (bf16[2,1024,1024]{2,1,0:T(8,128)(2,1)S(1)}, bf16[2,1024,1024]{2,1,0:T(8,128)(2,1)}, u32[]{:S(2)}) copy-start(bf16[2,1024,1024]{2,1,0:T(8,128)(2,1)} %fusion) | copy-start | bytes 12582916
  305.3 16.9 %slice-start.2 = ((s8[8388608]{0:T(1024)(128)(4,1)}), s8[4194304]{0:T(1024)(128)(4,1)S(1)}, s32[]{:S(2)}) async-start(s8[8388608]{0:T(1024)(128)(4,1)} %bitcast.110), calls=%async_computation.4 | async-start | bytes 8388608
  312.5 9.7 %slice-start.3 = ((s8[8388608]{0:T(1024)(128)(4,1)}), s8[4194304]{0:T(1024)(128)(4,1)S(1)}, s32[]{:S(2)}) async-start(s8[8388608]{0:T(1024)(128)(4,1)} %bitcast.110), calls=%async_computation.5 | async-start | bytes 8388608
  580.7 8.6 %copy-start.2 = (f32[1024,1024]{1,0:T(8,128)S(1)}, f32[1024,1024]{1,0:T(8,128)}, u32[]{:S(2)}) copy-start(f32[1024,1024]{1,0:T(8,128)} %get-tuple-element.50) | copy-start | bytes 12582916
  589.3 3.7 copy-start.1
Sparse Core Ops, SparseCore 0:
  99.5 117.6 all-reduce.4
  373.6 207.0 all-reduce.6
where the time goes:
time: 610 us; the launch traced here: 603 us
  waiting for transfers between devices  289 us (47%)
  blocking collectives  121 us (20%)
  matrix products  110 us (18%)
  local copies, waits for them, and re-layouts  41.6 us (7%)
  other arithmetic  22.9 us (4%)
  between operations  18.5 us (3%)
    psum x1, waiting for transfers between devices, local_step(): lax.psum((grad_one, grad_two, grad_three), 'data')  204 us
    psum x1, waiting for transfers between devices, local_step(): lax.psum((jnp.sum(z_views, axis=1, dtype=jnp.float32), jnp.einsum('woe,wo...  84.9 us
    psum x2, blocking collectives, local_step(): lax.psum((jnp.sum(z_views, axis=1, dtype=jnp.float32), jnp.einsum('woe,wo...  49.6 us
    psum x2, blocking collectives, layer_forward(): lax.psum(jnp.stack([jnp.sum(pre_act, axis=1), jnp.sum(pre_act * pre_act,...  48.8 us
    dot_general x2, matrix products, layer_forward(): jnp.einsum('vnk,kd->vnd', x_in, weight, preferred_element_type=jnp.float32)  25.6 us
    psum x1, blocking collectives, layer_backward(): lax.psum(jnp.stack([jnp.sum(d_act, axis=1), jnp.sum(d_act * normed, axis=...  22.7 us
    dot_general x1, matrix products, local_step(): jnp.einsum('vnf,vnd->fd', view_feats, d_pre_one, preferred_element_type=j...  17.4 us
    unnamed x33, local copies, waits for them, and re-layouts  16.4 us
  transfers between devices with their start and end apart: 2, of which 2 were waited for; matrix products, arithmetic and copies ran while one was open for 1% of the time, Pallas kernels for 0%

commit v1 on v0

v1 whole, which is shorter than its diff:
```python
import functools

import jax
import jax.numpy as jnp
from jax import lax
from jax.experimental import pallas as pl
from jax.experimental.pallas import tpu as pltpu
from jax.sharding import PartitionSpec as P

BN_EPS = 1e-5
STD_EPS = 1e-4
F32 = jnp.float32
BF16 = jnp.bfloat16
MESH = pl.DeviceIdType.MESH
NDEV = 8
BLK = 256
PAIRS = [(0, 0), (1, 1), (2, 2), (3, 3), (0, 1), (0, 2), (0, 3), (1, 2), (1, 3), (2, 3)]


class Place:
    def __init__(self):
        me = lax.axis_index('data')
        self.me = me
        self.c = lax.rem(me, 2)
        self.x = lax.rem(me // 2, 2)
        self.y = me // 4

    def flip(self, dy, dx, dc):
        y = 1 - self.y if dy else self.y
        x = 1 - self.x if dx else self.x
        c = 1 - self.c if dc else self.c
        return y * 4 + x * 2 + c

    def peer(self, o):
        return self.flip(o & 4, o & 2, o & 1)


def entry_barrier(place):
    barrier = pltpu.get_barrier_semaphore()
    for o in range(1, NDEV):
        pl.semaphore_signal(barrier, inc=1, device_id=(place.peer(o),), device_id_type=MESH)
    pl.semaphore_wait(barrier, NDEV - 1)


class StatExchange:
    def __init__(self, place, src, rcv, ssem, rsem):
        self.place, self.src, self.rcv, self.ssem, self.rsem = place, src, rcv, ssem, rsem
        self.sent = []

    def copies(self, slot):
        place = self.place
        return [pltpu.make_async_remote_copy(
            src_ref=self.src.at[slot], dst_ref=self.rcv.at[slot, place.me],
            send_sem=self.ssem.at[slot, o], recv_sem=self.rsem.at[slot, o],
            device_id=(place.peer(o),), device_id_type=MESH) for o in range(1, NDEV)]

    def send(self, slot):
        self.rcv[slot, self.place.me] = self.src[slot]
        for cp in self.copies(slot):
            cp.start()
        self.sent.append(slot)

    def total(self, slot):
        for cp in self.copies(slot):
            cp.wait_recv()
        acc = self.rcv[slot, 0]
        for d in range(1, NDEV):
            acc = acc + self.rcv[slot, d]
        return acc

    def drain(self):
        for slot in self.sent:
            for cp in self.copies(slot):
                cp.wait_send()


class Reduce:
    def __init__(self, place, part, full, rc, r1, r2, ssem, rsem):
        self.place, self.part, self.full = place, part, full
        self.rc, self.r1, self.r2 = rc, r1, r2
        self.ssem, self.rsem = ssem, rsem
        self.rows = part.shape[0]
        place_pq = [(place.x, place.y), (place.y, place.x)]
        rows, c = self.rows, place.c
        al = rows // 16
        self.leaf_rows = al
        mo = lambda v: pl.multiple_of(v, al)
        self.half_mine = mo(c * (rows // 2))
        self.half_other = mo((1 - c) * (rows // 2))
        self.o1_mine, self.o1_other, self.o2_mine, self.o2_other = [], [], [], []
        for k, (p, q) in enumerate(place_pq):
            base = c * (rows // 2) + k * (rows // 4)
            self.o1_mine.append(mo(base + p * (rows // 8)))
            self.o1_other.append(mo(base + (1 - p) * (rows // 8)))
            self.o2_mine.append(mo(base + p * (rows // 8) + q * (rows // 16)))
            self.o2_other.append(mo(base + p * (rows // 8) + (1 - q) * (rows // 16)))
        self.dev_c = place.flip(0, 0, 1)
        self.dev_1 = [place.flip(0, 1, 0), place.flip(1, 0, 0)]
        self.dev_2 = [place.flip(1, 0, 0), place.flip(0, 1, 0)]

    def _cp(self, idx, src, dst, dev):
        return pltpu.make_async_remote_copy(src_ref=src, dst_ref=dst, send_sem=self.ssem.at[idx], recv_sem=self.rsem.at[idx],
                                            device_id=(dev,), device_id_type=MESH)

    def cp_c(self):
        return [self._cp(0, self.part.at[pl.ds(self.half_other, self.rows // 2)], self.rc, self.dev_c)]

    def cp_1(self):
        return [self._cp(1 + k, self.part.at[pl.ds(self.o1_other[k], self.rows // 8)], self.r1.at[k], self.dev_1[k]) for k in (0, 1)]

    def cp_2(self):
        return [self._cp(3 + k, self.part.at[pl.ds(self.o2_other[k], self.rows // 16)], self.r2.at[k], self.dev_2[k]) for k in (0, 1)]

    def cp_g2(self):
        return [self._cp(5 + k, self.full.at[pl.ds(self.o2_mine[k], self.rows // 16)],
                         self.full.at[pl.ds(self.o2_mine[k], self.rows // 16)], self.dev_2[k]) for k in (0, 1)]

    def cp_g1(self):
        return [self._cp(7 + k, self.full.at[pl.ds(self.o1_mine[k], self.rows // 8)],
                         self.full.at[pl.ds(self.o1_mine[k], self.rows // 8)], self.dev_1[k]) for k in (0, 1)]

    def cp_gc(self):
        half = pl.ds(self.half_mine, self.rows // 2)
        return [self._cp(9, self.full.at[half], self.full.at[half], self.dev_c)]

    @staticmethod
    def start(cps):
        for cp in cps:
            cp.start()

    def begin(self):
        self.start(self.cp_c())

    def step_1(self):
        self.cp_c()[0].wait_recv()
        mine = pl.ds(self.half_mine, self.rows // 2)
        self.part[mine] = self.part[mine] + self.rc[...]
        self.start(self.cp_1())

    def step_2(self):
        for k, cp in enumerate(self.cp_1()):
            cp.wait_recv()
            mine = pl.ds(self.o1_mine[k], self.rows // 8)
            self.part[mine] = self.part[mine] + self.r1[k]
            self.cp_2()[k].start()

    def step_3(self, finish):
        for k, cp in enumerate(self.cp_2()):
            cp.wait_recv()
            mine = pl.ds(self.o2_mine[k], self.rows // 16)
            self.full[mine] = finish(self.o2_mine[k], self.part[mine] + self.r2[k])
            self.cp_g2()[k].start()

    def step_4(self):
        for k, cp in enumerate(self.cp_g2()):
            cp.wait_recv()
            self.cp_g1()[k].start()

    def step_5(self):
        for cp in self.cp_g1():
            cp.wait_recv()
        self.start(self.cp_gc())

    def step_6(self):
        self.cp_gc()[0].wait_recv()

    def drain(self):
        for cp in self.cp_c() + self.cp_1() + self.cp_2() + self.cp_g2() + self.cp_g1() + self.cp_gc():
            cp.wait_send()


def matmul_stats(dst, lhs, rhs, n_cols, store_stats):
    def body(j, _):
        cols = pl.ds(pl.multiple_of(j * BLK, BLK), BLK)
        out = jnp.dot(lhs[...], rhs[:, cols], preferred_element_type=F32)
        dst[:, cols] = out
        store_stats(cols, out)
        return 0

    lax.fori_loop(0, n_cols // BLK, body, 0)


def fwd_kernel(all_rows, h_a, h_b, w1, w2, w3, affine,
               n1_o, x1_o, n2_o, x2_o, dz_o, inv_o, loss_o,
               hbuf, w1b, w2b, w3b, u1, x1, u2, x2, gram, ghat, mu_outer, rc, r1, r2,
               st_src, st_rcv, zs_src, zs_rcv, ls_src, ls_rcv,
               ld_sem, out_sem, st_ss, st_rs, zs_ss, zs_rs, ls_ss, ls_rs, rd_ss, rd_rs):
    dim = w2b.shape[0]
    rows = u1.shape[1]
    packed = gram.shape[1]
    place = Place()

    loads = {}

    def load(name, src, dst):
        cp = pltpu.make_async_copy(src, dst, ld_sem.at[len(loads)])
        loads[name] = cp
        cp.start()

    load('w1', w1, w1b)
    load('ha', h_a, hbuf.at[0])
    load('hb', h_b, hbuf.at[1])
    load('w2', w2, w2b)
    load('w3', w3, w3b)
    outs = []

    def put(src, dst):
        cp = pltpu.make_async_copy(src, dst, out_sem.at[len(outs)])
        outs.append(cp)
        cp.start()

    entry_barrier(place)

    stats = StatExchange(place, st_src, st_rcv, st_ss, st_rs)
    zstats = StatExchange(place, zs_src, zs_rcv, zs_ss, zs_rs)
    lstats = StatExchange(place, ls_src, ls_rcv, ls_ss, ls_rs)

    def store_moments(slot):
        def store(cols, out):
            st_src[slot, 0:1, cols] = jnp.sum(out, axis=0, keepdims=True)
            st_src[slot, 1:2, cols] = jnp.sum(out * out, axis=0, keepdims=True)
        return store

    def norm_relu(slot, v, layer, ubuf, xbuf):
        mom = stats.total(slot)
        mean = mom[0:1] / all_rows
        var = mom[1:2] / all_rows - mean * mean
        inv = lax.rsqrt(var + BN_EPS)
        inv_o[2 * layer + v:2 * layer + v + 1, :] = inv
        gain = affine[2 * layer:2 * layer + 1, :]
        bias = affine[2 * layer + 1:2 * layer + 2, :]

        def body(i, _):
            rws = pl.ds(pl.multiple_of(i * 64, 64), 64)
            n = (ubuf[v, rws, :] - mean) * inv
            ubuf[v, rws, :] = n
            xbuf[v, rws, :] = jnp.maximum(gain * n + bias, 0.0).astype(BF16)
            return 0

        lax.fori_loop(0, rows // 64, body, 0)

    zcol = pl.ds(dim, dim)
    dzcol = pl.ds(0, dim)

    loads['w1'].wait()
    loads['ha'].wait()
    matmul_stats(u1.at[0], hbuf.at[0], w1b, dim, store_moments(0))
    stats.send(0)
    loads['hb'].wait()
    matmul_stats(u1.at[1], hbuf.at[1], w1b, dim, store_moments(1))
    stats.send(1)
    loads['w2'].wait()
    loads['w3'].wait()
    norm_relu(0, 0, 0, u1, x1)
    put(u1.at[0], n1_o.at[0])
    put(x1.at[0], x1_o.at[0])
    matmul_stats(u2.at[0], x1.at[0], w2b, dim, store_moments(2))
    stats.send(2)
    norm_relu(1, 1, 0, u1, x1)
    put(u1.at[1], n1_o.at[1])
    put(x1.at[1], x1_o.at[1])
    matmul_stats(u2.at[1], x1.at[1], w2b, dim, store_moments(3))
    stats.send(3)

    def project(v):
        def body(j, _):
            cols = pl.ds(pl.multiple_of(j * BLK, BLK), BLK)
            zc = pl.ds(pl.multiple_of(dim + j * BLK, BLK), BLK)
            z = jnp.dot(x2[v], w3b[:, cols], preferred_element_type=F32).astype(BF16)
            hbuf[v, :, zc] = z
            zf = z.astype(F32)
            zs_src[0, v:v + 1, cols] = jnp.sum(zf, axis=0, keepdims=True)
            if v == 1:
                diff = hbuf[0, :, zc].astype(F32) - zf
                zs_src[0, 2:3, cols] = jnp.sum(diff * diff, axis=0, keepdims=True)
                zs_src[0, 3:4, cols] = jnp.zeros((1, BLK), F32)
            return 0

        lax.fori_loop(0, dim // BLK, body, 0)

    def gram_of(v):
        for b, (i, j) in enumerate(PAIRS):
            zi = hbuf[v, :, dim + i * BLK:dim + (i + 1) * BLK]
            zj = hbuf[v, :, dim + j * BLK:dim + (j + 1) * BLK]
            gram[v, b * BLK:(b + 1) * BLK, :] = lax.dot_general(zi, zj, (((0,), (0,)), ((), ())), preferred_element_type=F32)

    reds = [Reduce(place, gram.at[v], ghat.at[v], rc.at[v], r1.at[v], r2.at[v], rd_ss.at[v], rd_rs.at[v]) for v in (0, 1)]

    norm_relu(2, 0, 1, u2, x2)
    put(u2.at[0], n2_o.at[0])
    put(x2.at[0], x2_o.at[0])
    project(0)
    gram_of(0)
    reds[0].begin()
    norm_relu(3, 1, 1, u2, x2)
    put(u2.at[1], n2_o.at[1])
    put(x2.at[1], x2_o.at[1])
    project(1)
    zstats.send(0)
    reds[0].step_1()
    gram_of(1)
    reds[1].begin()

    ztot = zstats.total(0)
    mus = [ztot[v:v + 1] / all_rows for v in (0, 1)]
    sq_sum = jnp.sum(ztot[2:3])
    for v in (0, 1):
        for b, (i, j) in enumerate(PAIRS):
            col = jnp.transpose(jnp.broadcast_to(mus[v][:, i * BLK:(i + 1) * BLK], (BLK, BLK)))
            mu_outer[v, b * BLK:(b + 1) * BLK, :] = (all_rows * col) * mus[v][:, j * BLK:(j + 1) * BLK]
    ls_src[0] = jnp.zeros((1, 128), F32)

    def finish(v):
        def fin(row, acc):
            leaf = reds[v].leaf_rows
            prow = row + lax.broadcasted_iota(jnp.int32, (leaf, BLK), 0)
            col = lax.broadcasted_iota(jnp.int32, (leaf, BLK), 1)
            diag_block = prow < 4 * BLK
            eye = diag_block & (lax.rem(prow, BLK) == col)
            cov = (acc - mu_outer[v, pl.ds(row, leaf), :]) / (all_rows - 1)
            std = jnp.sqrt(cov + STD_EPS)
            hinge = jnp.where(eye, jnp.maximum(1.0 - std, 0.0), 0.0)
            off = jnp.where(eye, 0.0, cov * cov) * jnp.where(diag_block, 1.0, 2.0)
            term = jnp.sum(hinge + 2.0 * off, axis=0, keepdims=True)
            ls_src[0] = ls_src[0] + term[:, :128] + term[:, 128:]
            on = jnp.where(std < 1.0, 1.0, 0.0)
            return jnp.where(eye, -on / (2.0 * std), 4.0 * cov).astype(BF16)
        return fin

    def expand(v):
        for b, (i, j) in enumerate(PAIRS):
            blk = ghat[v, b * BLK:(b + 1) * BLK, :]
            w1b[v * dim + i * BLK:v * dim + (i + 1) * BLK, j * BLK:(j + 1) * BLK] = blk
            if i != j:
                w1b[v * dim + j * BLK:v * dim + (j + 1) * BLK, i * BLK:(i + 1) * BLK] = jnp.transpose(blk)

    def grad_z(v):
        mu = mus[v]
        hi = mu.astype(BF16)
        mid = (mu - hi.astype(F32)).astype(BF16)
        low = (mu - hi.astype(F32) - mid.astype(F32)).astype(BF16)
        parts = jnp.concatenate([hi, mid, low, jnp.zeros((13, dim), BF16)], axis=0)
        sign = 1.0 if v == 0 else -1.0

        def body(j, _):
            cols = pl.ds(pl.multiple_of(j * BLK, BLK), BLK)
            zc = pl.ds(pl.multiple_of(dim + j * BLK, BLK), BLK)
            g = w1b[v * dim:(v + 1) * dim, cols]
            mean_part = jnp.sum(jnp.dot(parts, g, preferred_element_type=F32), axis=0, keepdims=True)
            row_part = jnp.dot(hbuf[v, :, zcol], g, preferred_element_type=F32)
            diff = hbuf[0, :, zc].astype(F32) - hbuf[1, :, zc].astype(F32)
            dz = (2.0 / (all_rows - 1)) * (row_part - mean_part) + (sign * 4.0 / all_rows) * diff
            hbuf[v, :, cols] = dz.astype(BF16)
            return 0

        lax.fori_loop(0, dim // BLK, body, 0)
        put(hbuf.at[v, :, dzcol], dz_o.at[v])

    reds[1].step_1()
    reds[0].step_2()
    reds[1].step_2()
    reds[0].step_3(finish(0))
    reds[1].step_3(finish(1))
    lstats.send(0)
    reds[0].step_4()
    reds[0].step_5()
    reds[1].step_4()
    reds[0].step_6()
    expand(0)
    grad_z(0)
    reds[1].step_5()
    reds[1].step_6()
    expand(1)
    grad_z(1)
    loss_o[...] = jnp.broadcast_to(jnp.sum(lstats.total(0)) + 2.0 * sq_sum / all_rows, (8, 128))
    for ex in (stats, zstats, lstats):
        ex.drain()
    for red in reds:
        red.drain()
    for cp in outs:
        cp.wait()


def forward(n_dev, h_a, h_b, w1, w2, w3, affine):
    rows, feat = h_a.shape
    dim = w2.shape[0]
    all_rows = rows * n_dev
    packed = len(PAIRS) * BLK
    any_spec = pl.BlockSpec(memory_space=pl.ANY)
    vm = pl.BlockSpec(memory_space=pltpu.VMEM)
    wide = lambda dt: jax.ShapeDtypeStruct((2, rows, dim), dt)
    dma = pltpu.SemaphoreType.DMA
    return pl.pallas_call(
        functools.partial(fwd_kernel, all_rows),
        name='forward',
        out_shape=[wide(F32), wide(BF16), wide(F32), wide(BF16), wide(BF16),
                   jax.ShapeDtypeStruct((4, dim), F32), jax.ShapeDtypeStruct((8, 128), F32)],
        in_specs=[any_spec] * 5 + [vm],
        out_specs=[any_spec] * 5 + [vm, vm],
        scratch_shapes=[
            pltpu.VMEM((2, rows, feat), BF16), pltpu.VMEM((feat, dim), BF16), pltpu.VMEM((dim, dim), BF16), pltpu.VMEM((dim, dim), BF16),
            pltpu.VMEM((2, rows, dim), F32), pltpu.VMEM((2, rows, dim), BF16), pltpu.VMEM((2, rows, dim), F32), pltpu.VMEM((2, rows, dim), BF16),
            pltpu.VMEM((2, packed, BLK), F32), pltpu.VMEM((2, packed, BLK), BF16), pltpu.VMEM((2, packed, BLK), F32),
            pltpu.VMEM((2, packed // 2, BLK), F32), pltpu.VMEM((2, 2, packed // 8, BLK), F32), pltpu.VMEM((2, 2, packed // 16, BLK), F32),
            pltpu.VMEM((4, 2, dim), F32), pltpu.VMEM((4, NDEV, 2, dim), F32),
            pltpu.VMEM((1, 4, dim), F32), pltpu.VMEM((1, NDEV, 4, dim), F32),
            pltpu.VMEM((1, 1, 128), F32), pltpu.VMEM((1, NDEV, 1, 128), F32),
            dma((5,)), dma((10,)), dma((4, NDEV)), dma((4, NDEV)), dma((1, NDEV)), dma((1, NDEV)), dma((1, NDEV)), dma((1, NDEV)),
            dma((2, 10)), dma((2, 10))],
        compiler_params=pltpu.CompilerParams(collective_id=0, has_side_effects=True, vmem_limit_bytes=67043328),
    )(h_a, h_b, w1, w2, w3, affine)


def solution(mesh):
    n_dev = mesh.shape['data']

    def local_step(h_a, h_b, w_one, w_two, w_three, gain_one, bias_one, gain_two, bias_two):
        all_rows = h_a.shape[0] * n_dev
        affine = jnp.stack([gain_one, bias_one, gain_two, bias_two])
        norm1, x1, norm2, x2, d_z, inv, loss = forward(n_dev, h_a, h_b, w_one, w_two, w_three, affine)
        grad_three = jnp.einsum('vnk,vnd->kd', x2, d_z, preferred_element_type=F32)
        d_x2 = jnp.einsum('vnd,kd->vnk', d_z, w_three, preferred_element_type=F32)
        d_u2, d_gain_two, d_bias_two = layer_backward(d_x2, norm2, inv[2:4, None, :], gain_two, bias_two, all_rows)
        grad_two = jnp.einsum('vnk,vnd->kd', x1, d_u2, preferred_element_type=F32)
        d_x1 = jnp.einsum('vnd,kd->vnk', d_u2, w_two, preferred_element_type=F32)
        d_u1, d_gain_one, d_bias_one = layer_backward(d_x1, norm1, inv[0:2, None, :], gain_one, bias_one, all_rows)
        grad_one = (jnp.einsum('nf,nd->fd', h_a, d_u1[0], preferred_element_type=F32)
                    + jnp.einsum('nf,nd->fd', h_b, d_u1[1], preferred_element_type=F32))
        grad_one, grad_two, grad_three = lax.psum((grad_one, grad_two, grad_three), 'data')
        return loss[0, 0], grad_one, grad_two, grad_three, d_gain_one, d_bias_one, d_gain_two, d_bias_two

    row = P('data', None)
    return jax.shard_map(local_step, mesh=mesh, in_specs=(row, row) + (P(),) * 7, out_specs=(P(),) * 8, check_vma=False)


def layer_backward(d_out, normed, inv_std, gain_vec, bias_vec, all_rows):
    d_act = jnp.where(gain_vec * normed + bias_vec > 0.0, d_out, 0.0)
    sums = lax.psum(jnp.stack([jnp.sum(d_act, axis=1), jnp.sum(d_act * normed, axis=1)]), 'data')
    d_pre = inv_std * gain_vec * (d_act - sums[0][:, None, :] / all_rows - normed * (sums[1][:, None, :] / all_rows))
    return d_pre.astype(BF16), jnp.sum(sums[1], axis=0), jnp.sum(sums[0], axis=0)
```

time: 610 us -> 432 us (0.71)
  Pallas kernels: 0 us -> 82.4 us
  waiting for transfers between devices: 289 us -> 207 us
  blocking collectives: 121 us -> 45.7 us
  matrix products: 110 us -> 46.4 us
  local copies, waits for them, and re-layouts: 41.6 us -> 17.4 us
    psum x4 -> x0, blocking collectives: 98.4 us -> none  [the longest x2 49.6 us: local_step(): lax.psum((jnp.sum(z_views, axis=1, dtype=jnp.float32), jnp.einsum('woe,wo...]
    psum x1 -> x0, waiting for transfers between devices: 84.9 us -> none  [local_step(): lax.psum((jnp.sum(z_views, axis=1, dtype=jnp.float32), jnp.einsum('woe,wo...]
    pallas_call x0 -> x1, Pallas kernels: none -> 82.4 us  [forward(): pl.pallas_call(functools.partial(fwd_kernel, all_rows), name='forward', o...]
    dot_general x11 -> x6, matrix products: 110 us -> 46.4 us  [the longest x1 10.2 us: local_step(): d_x1 = jnp.einsum('vnd,kd->vnk', d_u2, w_two, preferred_element_type=F32)]
    psum x1 -> x2, blocking collectives: 22.7 us -> 45.7 us  [layer_backward(): lax.psum(jnp.stack([jnp.sum(d_act, axis=1), jnp.sum(d_act * normed, axis=...]
    div x1 -> x0, local copies, waits for them, and re-layouts: 12.9 us -> none  [loss_from_stats(): (gram_mat - all_rows * col_mu[:, :, None] * col_mu[:, None, :]) / (all_ro...]
    gather x1 -> x0, local copies, waits for them, and re-layouts: 12.3 us -> none  [loss_from_stats(): diag_var = jnp.diagonal(cov_mat, axis1=1, axis2=2)]
    mul x1 -> x0, other arithmetic: 7.54 us -> none  [loss_from_stats(): d_inv = 2.0 * INV_WEIGHT / all_rows * z_diff]
  transfers between devices with their start and end apart: 2 -> 1, of which waited for: 2 -> 1; matrix products, arithmetic and copies ran while one was open for 1% -> 0% of each run, Pallas kernels for 0% -> 0%
where the time goes in v1:
time: 432 us; the launch traced here: 431 us
  waiting for transfers between devices  207 us (48%)
  Pallas kernels  82.4 us (19%)
  matrix products  46.4 us (11%)
  blocking collectives  45.7 us (11%)
  other arithmetic  17.9 us (4%)
  local copies, waits for them, and re-layouts  17.4 us (4%)
  between operations  14.2 us (3%)
    psum x1, waiting for transfers between devices, local_step(): lax.psum((grad_one, grad_two, grad_three), 'data')  207 us
    pallas_call x1, Pallas kernels, forward(): pl.pallas_call(functools.partial(fwd_kernel, all_rows), name='forward', o...  82.4 us
    psum x2, blocking collectives, layer_backward(): lax.psum(jnp.stack([jnp.sum(d_act, axis=1), jnp.sum(d_act * normed, axis=...  45.7 us
    unnamed x27, local copies, waits for them, and re-layouts  16.3 us
    convert_element_type x2, other arithmetic, layer_backward(): d_pre.astype(BF16)  14.4 us
    dot_general x1, matrix products, local_step(): d_x1 = jnp.einsum('vnd,kd->vnk', d_u2, w_two, preferred_element_type=F32)  10.2 us
    dot_general x1, matrix products, local_step(): grad_three = jnp.einsum('vnk,vnd->kd', x2, d_z, preferred_element_type=F32)  10.2 us
  transfers between devices with their start and end apart: 1, of which 1 were waited for; matrix products, arithmetic and copies ran while one was open for 0% of the time, Pallas kernels for 0%

profile of v1, /device:TPU:0, one launch (start us, length us, event | category | flops | bytes accessed | tf_op | source)
XLA Modules:
  0.0 431.1 jit_solution(15170730789511553417)
XLA Ops:
  7.2 0.0 all-reduce.3.cloned.1.call-start
  7.2 1.4 pad_maximum_fusion.affine
  8.6 82.4 %forward.1 = (f32[2,1024,1024]{2,1,0:T(8,128)}, bf16[2,1024,1024]{2,1,0:T(8,128)(2,1)}, f32[2,1024,1024]{2,1,0:T(8,128)}, bf16[2,1024,1024]{2,1,0:T(8,128)(2,1)}...) custom-call(bf16[1024,2048]{1,0:T(8,128)(2,1)} %h_a.1, bf16[1024,2048]{1,0:T(8,128)(2,1)} %h_b.1, ...), custom_call_target="tpu_custom_call" | custom-call | tf_op jit(solution)/shard_map/forward/pallas_call | solution.py:393
  91.0 0.8 slice_multiply_fusion.1
  91.8 0.0 copy-start.4
  91.8 0.0 copy-start.6
  91.9 0.0 copy-start.8
  91.9 0.0 copy-start.11
  91.9 10.2 %convolution_bitcast_fusion = f32[1024,1024]{1,0:T(8,128)} fusion(bf16[2,1024,1024]{2,1,0:T(8,128)(2,1)} %get-tuple-element.21, bf16[2,1024,1024]{2,1,0:T(8,128)(2,1)} %get-tuple-element.19), kind=kOutput, calls=%fused_computation.11 | convolution fusion | flops 4294967296 | bytes 12582912 | tf_op jit(solution)/shard_map/vnk,vnd->kd/dot_general | solution.py:421
  102.1 0.0 copy-done
  102.1 8.0 %fusion.2 = (f32[2,1024]{1,0:T(2,128)S(1)}, f32[2,1024]{1,0:T(2,128)S(1)}, f32[2,1024,1024]{2,1,0:T(8,128)}) fusion(f32[2,1024,1024]{2,1,0:T(8,128)S(1)} %copy-done, f32[1024]{0:T(1024)S(1)} %copy-done.8, f32[1024]{0:T(1024)S(1)} %copy-done.6, bf16[2,1024,1024]{2,1,0:T(8,128)(2,1)S(1)} %copy-done.11, bf16[1024,1024]{1,0:T(8,128)(2,1)S(1)} %copy-done.4), kind=kOutput, calls=%fused_computation.9 | convolution fusion | flops 4309643264 | bytes 23093248 | tf_op jit(solution)/shard_map/vnd,kd->vnk/dot_general | solution.py:422
  110.1 22.3 %psum.35 = f32[2,2,1024]{2,1,0:T(2,128)S(1)} all-reduce(f32[2,2,1024]{2,1,0:T(2,128)S(1)} %pad_maximum_fusion.1), channel_id=1, replica_groups=mesh['data'=8] {'data'}, use_global_device_ids=true, to_apply=%region_2.3 | all-reduce | flops 4096 | bytes 32768 | tf_op jit(solution)/shard_map/psum | solution.py:438
  132.5 0.6 slice_reduce_fusion.3
  133.1 7.2 %multiply_convert_fusion.1 = bf16[2,1024,1024]{2,1,0:T(8,128)(2,1)S(1)} fusion(f32[2,1024,1024]{2,1,0:T(8,128)} %get-tuple-element.18, f32[2,1024,1024]{2,1,0:T(8,128)} %get-tuple-element.47, f32[2,1024]{1,0:T(2,128)S(1)} %get-tuple-element.41, f32[2,1024]{1,0:T(2,128)S(1)} %get-tuple-element.42, f32[1024]{0:T(1024)S(1)} %copy-done.8, f32[1024]{0:T(1024)S(1)} %copy-done.6, ...), kind=kLoop, calls=%fused_computation.3 | loop fusion | flops 18874368 | bytes 21004288 | tf_op jit(solution)/shard_map/convert_element_type | solution.py:440
  140.3 0.0 copy-done.10
  140.3 0.0 copy-start.5
  140.3 0.0 copy-start.7
  140.3 0.0 copy-start.9
  140.4 6.1 %convolution_bitcast_fusion.1 = f32[1024,1024]{1,0:T(8,128)} fusion(bf16[2,1024,1024]{2,1,0:T(8,128)(2,1)S(1)} %copy-done.10, bf16[2,1024,1024]{2,1,0:T(8,128)(2,1)S(1)} %multiply_convert_fusion.1), kind=kOutput, calls=%fused_computation.12 | convolution fusion | flops 4294967296 | bytes 12582912 | tf_op jit(solution)/shard_map/vnk,vnd->kd/dot_general | solution.py:424
  146.5 10.2 %fusion.3 = (f32[2,1024]{1,0:T(2,128)S(1)}, f32[2,1024]{1,0:T(2,128)S(1)}, f32[2,1024,1024]{2,1,0:T(8,128)}) fusion(f32[2,1024,1024]{2,1,0:T(8,128)} %get-tuple-element.17, f32[1024]{0:T(1024)S(1)} %copy-done.9, f32[1024]{0:T(1024)S(1)} %copy-done.7, bf16[2,1024,1024]{2,1,0:T(8,128)(2,1)S(1)} %multiply_convert_fusion.1, bf16[1024,1024]{1,0:T(8,128)(2,1)S(1)} %copy-done.5), kind=kOutput, calls=%fused_computation.10 | convolution fusion | flops 4309643264 | bytes 23093248 | tf_op jit(solution)/shard_map/vnd,kd->vnk/dot_general | solution.py:425
  156.7 23.3 %psum.36 = f32[2,2,1024]{2,1,0:T(2,128)S(1)} all-reduce(f32[2,2,1024]{2,1,0:T(2,128)S(1)} %pad_maximum_fusion.2), channel_id=1, replica_groups=mesh['data'=8] {'data'}, use_global_device_ids=true, to_apply=%region_5.6 | all-reduce | flops 4096 | bytes 32768 | tf_op jit(solution)/shard_map/psum | solution.py:438
  180.0 0.6 slice_reduce_fusion.1
  180.6 7.2 %multiply_convert_fusion = bf16[2,1024,1024]{2,1,0:T(8,128)(2,1)S(1)} fusion(f32[2,1024,1024]{2,1,0:T(8,128)} %get-tuple-element.17, f32[2,1024,1024]{2,1,0:T(8,128)} %get-tuple-element.48, f32[2,1024]{1,0:T(2,128)S(1)} %get-tuple-element.43, f32[2,1024]{1,0:T(2,128)S(1)} %get-tuple-element.44, f32[1024]{0:T(1024)S(1)} %copy-done.9, f32[1024]{0:T(1024)S(1)} %copy-done.7, ...), kind=kLoop, calls=%fused_computation.1 | loop fusion | flops 18874368 | bytes 21004288 | tf_op jit(solution)/shard_map/convert_element_type | solution.py:440
  187.9 0.0 copy-start.2
  187.9 4.7 %fusion.4 = f32[1024,2048]{1,0:T(8,128)S(1)} fusion(bf16[1024,2048]{1,0:T(8,128)(2,1)S(1)} %copy-done.1, bf16[2,1024,1024]{2,1,0:T(8,128)(2,1)S(1)} %multiply_convert_fusion), kind=kOutput, calls=%fused_computation.15 | convolution fusion | flops 4294967296 | bytes 14680064 | tf_op jit(solution)/shard_map/nf,nd->fd/dot_general | solution.py:427
  192.6 7.2 %add_bitcast_fusion = f32[2048,1024]{0,1:T(8,128)} fusion(f32[1024,2048]{1,0:T(8,128)S(1)} %fusion.4, bf16[1024,2048]{1,0:T(8,128)(2,1)S(1)} %copy-done.2, bf16[2,1024,1024]{2,1,0:T(8,128)(2,1)S(1)} %multiply_convert_fusion), kind=kOutput, calls=%fused_computation | convolution fusion | flops 4297064448 | bytes 23068672 | tf_op jit(solution)/shard_map/nf,nd->fd/dot_general | solution.py:428
  199.8 0.0 all-reduce.3.cloned.1.call-update
  199.8 1.2 slice.31
  201.0 207.0 %all-reduce.3.cloned.1.call-done = (f32[2048,1024]{0,1:T(8,128)}, f32[1024,1024]{1,0:T(8,128)}, f32[1024,1024]{1,0:T(8,128)}) async-done(((f32[2048,1024]{0,1:T(8,128)}, f32[1024,1024]{1,0:T(8,128)}, f32[1024,1024]{1,0:T(8,128)}), (f32[2048,1024]{0,1:T(8,128)}, f32[1024,1024]{1,0:T(8,128)}, f32[1024,1024]{1,0:T(8,128)})) %all-reduce.3.cloned.1.call-update) | async-done | bytes 16777232 | tf_op jit(solution)/shard_map/psum | solution.py:429
  408.1 9.2 %copy.19 = f32[2048,1024]{1,0:T(8,128)} copy(f32[2048,1024]{0,1:T(8,128)} %get-tuple-element.38) | data formatting | bytes 16777216
  417.3 4.9 %copy.25 = f32[1024,1024]{1,0:T(8,128)} copy(f32[1024,1024]{1,0:T(8,128)} %get-tuple-element.51) | data formatting | bytes 8388608
  422.2 2.0 copy.26
  (16 shorter events, 0.0 us)
Async XLA Ops:
  7.2 400.9 %all-reduce.3.cloned.1.call-start = ((), (), s32[]{:S(2)}) async-start(), calls=%async_computation | async-start | bytes 33554432 | tf_op jit(solution)/shard_map/psum | solution.py:429
  91.8 10.2 %copy-start = (f32[2,1024,1024]{2,1,0:T(8,128)S(1)}, f32[2,1024,1024]{2,1,0:T(8,128)}, u32[]{:S(2)}) copy-start(f32[2,1024,1024]{2,1,0:T(8,128)} %get-tuple-element.18) | copy-start | bytes 25165828
  91.8 10.2 %copy-start.4 = (bf16[1024,1024]{1,0:T(8,128)(2,1)S(1)}, bf16[1024,1024]{1,0:T(8,128)(2,1)}, u32[]{:S(2)}) copy-start(bf16[1024,1024]{1,0:T(8,128)(2,1)} %w3.1) | copy-start | bytes 6291460
  91.8 10.2 %copy-start.6 = (f32[1024]{0:T(1024)S(1)}, f32[1024]{0:T(1024)}, u32[]{:S(2)}) copy-start(f32[1024]{0:T(1024)} %param.16) | copy-start | bytes 12292
  91.9 10.2 %copy-start.8 = (f32[1024]{0:T(1024)S(1)}, f32[1024]{0:T(1024)}, u32[]{:S(2)}) copy-start(f32[1024]{0:T(1024)} %param.17) | copy-start | bytes 12292
  91.9 10.2 %copy-start.11 = (bf16[2,1024,1024]{2,1,0:T(8,128)(2,1)S(1)}, bf16[2,1024,1024]{2,1,0:T(8,128)(2,1)}, u32[]{:S(2)}) copy-start(bf16[2,1024,1024]{2,1,0:T(8,128)(2,1)} %get-tuple-element.19) | copy-start | bytes 12582916
  133.1 7.2 %copy-start.10 = (bf16[2,1024,1024]{2,1,0:T(8,128)(2,1)S(1)}, bf16[2,1024,1024]{2,1,0:T(8,128)(2,1)}, u32[]{:S(2)}) copy-start(bf16[2,1024,1024]{2,1,0:T(8,128)(2,1)} %get-tuple-element.20) | copy-start | bytes 12582916
  140.3 6.1 %copy-start.5 = (bf16[1024,1024]{1,0:T(8,128)(2,1)S(1)}, bf16[1024,1024]{1,0:T(8,128)(2,1)}, u32[]{:S(2)}) copy-start(bf16[1024,1024]{1,0:T(8,128)(2,1)} %w2.1) | copy-start | bytes 6291460
  140.3 6.1 %copy-start.7 = (f32[1024]{0:T(1024)S(1)}, f32[1024]{0:T(1024)}, u32[]{:S(2)}) copy-start(f32[1024]{0:T(1024)} %param.14) | copy-start | bytes 12292
  140.3 6.1 %copy-start.9 = (f32[1024]{0:T(1024)S(1)}, f32[1024]{0:T(1024)}, u32[]{:S(2)}) copy-start(f32[1024]{0:T(1024)} %param.15) | copy-start | bytes 12292
  180.6 7.2 %copy-start.1 = (bf16[1024,2048]{1,0:T(8,128)(2,1)S(1)}, bf16[1024,2048]{1,0:T(8,128)(2,1)}, u32[]{:S(2)}) copy-start(bf16[1024,2048]{1,0:T(8,128)(2,1)} %h_a.1) | copy-start | bytes 12582916
  187.9 4.7 %copy-start.2 = (bf16[1024,2048]{1,0:T(8,128)(2,1)S(1)}, bf16[1024,2048]{1,0:T(8,128)(2,1)}, u32[]{:S(2)}) copy-start(bf16[1024,2048]{1,0:T(8,128)(2,1)} %h_b.1) | copy-start | bytes 12582916
  417.3 4.9 %copy-start.3 = (f32[1024,1024]{1,0:T(8,128)S(1)}, f32[1024,1024]{1,0:T(8,128)}, u32[]{:S(2)}) copy-start(f32[1024,1024]{1,0:T(8,128)} %get-tuple-element.52) | copy-start | bytes 12582916
Sparse Core Ops, SparseCore 0:
  199.9 208.0 all-reduce.2

commit v2 on v1

v2 whole, which is shorter than its diff:
```python
import functools

import jax
import jax.numpy as jnp
from jax import lax
from jax.experimental import pallas as pl
from jax.experimental.pallas import tpu as pltpu
from jax.sharding import PartitionSpec as P

BN_EPS = 1e-5
STD_EPS = 1e-4
F32 = jnp.float32
BF16 = jnp.bfloat16
MESH = pl.DeviceIdType.MESH
NDEV = 8
BLK = 256
STRIP = 64
SPARE = 524288
ROWS = 512
VMEM_BYTES = 67043328
LANES = 128
QUAD = 128
DIAG_ROWS = 4 * QUAD
TRI_ROWS = 6 * QUAD
OFF_PAIRS = [(0, 1), (0, 2), (0, 3), (1, 2), (1, 3), (2, 3)]
PIECES = []
for _i in range(4):
    _b = _i * BLK
    PIECES += [(_i * QUAD, 0, _b, _b, QUAD, False), (_i * QUAD, QUAD, _b, _b + QUAD, QUAD, True),
               (DIAG_ROWS + _i // 2 * QUAD, _i % 2 * QUAD, _b + QUAD, _b + QUAD, QUAD, False)]
PIECES += [(TRI_ROWS + _b * BLK, 0, _i * BLK, _j * BLK, BLK, True) for _b, (_i, _j) in enumerate(OFF_PAIRS)]
PACKED = TRI_ROWS + len(OFF_PAIRS) * BLK
SPLIT = TRI_ROWS + 2 * BLK
SPANS = ((0, SPLIT), (SPLIT, PACKED))
ROW0, ROW1 = slice(0, 1), slice(1, 2)
TN = (((0,), (0,)), ((), ()))
NT = (((1,), (1,)), ((), ()))


def dot(a, b, dims=(((1,), (0,)), ((), ()))):
    return lax.dot_general(a, b, dims, preferred_element_type=F32)


def col_sum(v):
    return jnp.sum(v, axis=0, keepdims=True)


def one(i):
    return slice(i, i + 1)


def tile(j, size=BLK, base=0):
    return pl.ds(pl.multiple_of(base + j * size, size), size)


def span(i, base=0):
    return slice(base + i * BLK, base + i * BLK + BLK)


def loop(count, body):
    def step(i, carry):
        body(i)
        return carry

    lax.fori_loop(0, count, step, 0)


class Place:
    def __init__(self):
        me = lax.axis_index('data')
        self.me = me
        self.c = lax.rem(me, 2)
        self.x = lax.rem(me // 2, 2)
        self.y = me // 4

    def flip(self, dy, dx, dc):
        y = 1 - self.y if dy else self.y
        x = 1 - self.x if dx else self.x
        c = 1 - self.c if dc else self.c
        return y * 4 + x * 2 + c

    def peer(self, o):
        return self.flip(o & 4, o & 2, o & 1)


def entry_barrier(place):
    barrier = pltpu.get_barrier_semaphore()
    for o in range(1, NDEV):
        pl.semaphore_signal(barrier, inc=1, device_id=(place.peer(o),), device_id_type=MESH)
    pl.semaphore_wait(barrier, NDEV - 1)


class StatExchange:
    def __init__(self, place, src, rcv, ssem, rsem):
        self.place, self.src, self.rcv, self.ssem, self.rsem = place, src, rcv, ssem, rsem
        self.sent = []

    def copies(self, slot):
        place = self.place
        return [pltpu.make_async_remote_copy(
            src_ref=self.src.at[slot], dst_ref=self.rcv.at[slot, place.me],
            send_sem=self.ssem.at[slot, o], recv_sem=self.rsem.at[slot, o],
            device_id=(place.peer(o),), device_id_type=MESH) for o in range(1, NDEV)]

    def send(self, slot):
        self.rcv[slot, self.place.me] = self.src[slot]
        for cp in self.copies(slot):
            cp.start()
        self.sent.append(slot)

    def total(self, slot):
        for cp in self.copies(slot):
            cp.wait_recv()
        acc = self.rcv[slot, 0]
        for d in range(1, NDEV):
            acc = acc + self.rcv[slot, d]
        return acc

    def drain(self):
        for slot in self.sent:
            for cp in self.copies(slot):
                cp.wait_send()


class Reduce:
    def __init__(self, place, part, full, rc, r1, r2, ssem, rsem):
        self.place, self.part, self.full = place, part, full
        self.ssem, self.rsem = ssem, rsem
        self.rows = part.shape[0]
        self.rc = rc.at[pl.ds(0, self.rows // 2)]
        self.r1 = [r1.at[k, pl.ds(0, self.rows // 8)] for k in (0, 1)]
        self.r2 = [r2.at[k, pl.ds(0, self.rows // 16)] for k in (0, 1)]
        place_pq = [(place.x, place.y), (place.y, place.x)]
        rows, c = self.rows, place.c
        al = rows // 16
        self.leaf_rows = al
        mo = lambda v: pl.multiple_of(v, al)
        self.half_mine = mo(c * (rows // 2))
        self.half_other = mo((1 - c) * (rows // 2))
        self.o1_mine, self.o1_other, self.o2_mine, self.o2_other = [], [], [], []
        for k, (p, q) in enumerate(place_pq):
            base = c * (rows // 2) + k * (rows // 4)
            self.o1_mine.append(mo(base + p * (rows // 8)))
            self.o1_other.append(mo(base + (1 - p) * (rows // 8)))
            self.o2_mine.append(mo(base + p * (rows // 8) + q * (rows // 16)))
            self.o2_other.append(mo(base + p * (rows // 8) + (1 - q) * (rows // 16)))
        self.dev_c = place.flip(0, 0, 1)
        self.dev_1 = [place.flip(0, 1, 0), place.flip(1, 0, 0)]
        self.dev_2 = [place.flip(1, 0, 0), place.flip(0, 1, 0)]

    def _cp(self, idx, src, dst, dev):
        return pltpu.make_async_remote_copy(src_ref=src, dst_ref=dst, send_sem=self.ssem.at[idx], recv_sem=self.rsem.at[idx],
                                            device_id=(dev,), device_id_type=MESH)

    def cp_c(self):
        return [self._cp(0, self.part.at[pl.ds(self.half_other, self.rows // 2)], self.rc, self.dev_c)]

    def cp_1(self):
        return [self._cp(1 + k, self.part.at[pl.ds(self.o1_other[k], self.rows // 8)], self.r1[k], self.dev_1[k]) for k in (0, 1)]

    def cp_2(self):
        return [self._cp(3 + k, self.part.at[pl.ds(self.o2_other[k], self.rows // 16)], self.r2[k], self.dev_2[k]) for k in (0, 1)]

    def cp_g2(self):
        return [self._cp(5 + k, self.full.at[pl.ds(self.o2_mine[k], self.rows // 16)],
                         self.full.at[pl.ds(self.o2_mine[k], self.rows // 16)], self.dev_2[k]) for k in (0, 1)]

    def cp_g1(self):
        return [self._cp(7 + k, self.full.at[pl.ds(self.o1_mine[k], self.rows // 8)],
                         self.full.at[pl.ds(self.o1_mine[k], self.rows // 8)], self.dev_1[k]) for k in (0, 1)]

    def cp_gc(self):
        half = pl.ds(self.half_mine, self.rows // 2)
        return [self._cp(9, self.full.at[half], self.full.at[half], self.dev_c)]

    @staticmethod
    def start(cps):
        for cp in cps:
            cp.start()

    def begin(self):
        self.start(self.cp_c())

    def step_1(self):
        self.cp_c()[0].wait_recv()
        mine = pl.ds(self.half_mine, self.rows // 2)
        self.part[mine] = self.part[mine] + self.rc[...]
        self.start(self.cp_1())

    def step_2(self):
        for k, (cp, nxt) in enumerate(zip(self.cp_1(), self.cp_2())):
            cp.wait_recv()
            mine = pl.ds(self.o1_mine[k], self.rows // 8)
            self.part[mine] = self.part[mine] + self.r1[k][...]
            nxt.start()

    def step_3(self, finish):
        for k, (cp, nxt) in enumerate(zip(self.cp_2(), self.cp_g2())):
            cp.wait_recv()
            mine = pl.ds(self.o2_mine[k], self.rows // 16)
            self.full[mine] = finish(self.o2_mine[k], self.part[mine] + self.r2[k][...])
            nxt.start()

    def step_4(self):
        for cp in self.cp_g2():
            cp.wait_recv()
        self.start(self.cp_g1())

    def step_5(self):
        for cp in self.cp_g1():
            cp.wait_recv()
        self.start(self.cp_gc())

    def step_6(self):
        self.cp_gc()[0].wait_recv()

    def drain(self):
        for cp in self.cp_c() + self.cp_1() + self.cp_2() + self.cp_g2() + self.cp_g1() + self.cp_gc():
            cp.wait_send()


GramReduce = Reduce


def by_rows(lhs, rhs, use, sums=0, dims=(((1,), (0,)), ((), ()))):
    def step(i, carry):
        rws = tile(i, ROWS)
        terms = use(rws, dot(lhs[rws, :], rhs[...], dims))
        return tuple(c + col_sum(t) for c, t in zip(carry, terms))

    width = rhs.shape[1 - dims[0][1][0]]
    return lax.fori_loop(0, lhs.shape[0] // ROWS, step, (jnp.zeros((1, width), F32),) * sums)


def fwd_kernel(all_rows, h_a, h_b, w1, w2, w3, g1, b1, g2, b2,
               n1_o, x1_o, n2_o, x2_o, dz_o, inv_o, loss_o,
               hbuf, w1b, w2b, w3b, u1, x1, u2, x2, gram, ghat, mu_outer, rc, r1, r2,
               st_src, st_rcv, zs_src, zs_rcv, ls_src, ls_rcv,
               ld_sem, out_sem, st_ss, st_rs, zs_ss, zs_rs, ls_ss, ls_rs, rd_ss, rd_rs):
    dim = w2b.shape[0]
    rows = u1.shape[1]
    affine = ((g1, b1), (g2, b2))
    place = Place()

    loads = {}

    def load(name, src, dst):
        cp = pltpu.make_async_copy(src, dst, ld_sem.at[len(loads)])
        loads[name] = cp
        cp.start()

    load('w1', w1, w1b)
    load('ha', h_a, hbuf.at[0])
    load('hb', h_b, hbuf.at[1])
    load('w2', w2, w2b)
    load('w3', w3, w3b)
    outs = []

    def put(src, dst):
        cp = pltpu.make_async_copy(src, dst, out_sem.at[len(outs)])
        outs.append(cp)
        cp.start()

    entry_barrier(place)

    stats = StatExchange(place, st_src, st_rcv, st_ss, st_rs)
    zstats = StatExchange(place, zs_src, zs_rcv, zs_ss, zs_rs)
    lstats = StatExchange(place, ls_src, ls_rcv, ls_ss, ls_rs)

    def linear(slot, dst, lhs, rhs):
        def use(rws, out):
            dst[rws, :] = out
            return out, out * out

        st_src[slot, ROW0, :], st_src[slot, ROW1, :] = by_rows(lhs, rhs, use, 2)
        stats.send(slot)

    def norm_relu(slot, v, layer, ubuf, xbuf):
        mom = stats.total(slot)
        mean = mom[ROW0] / all_rows
        var = mom[ROW1] / all_rows - mean * mean
        inv = lax.rsqrt(var + BN_EPS)
        inv_o[one(slot), :] = inv
        gain, bias = affine[layer]

        def body(i):
            rws = tile(i, STRIP)
            n = (ubuf[v, rws, :] - mean) * inv
            ubuf[v, rws, :] = n
            xbuf[v, rws, :] = jnp.maximum(gain[...] * n + bias[...], 0.0).astype(BF16)

        loop(rows // STRIP, body)

    zcol = pl.ds(dim, dim)
    dzcol = pl.ds(0, dim)
    zb = [hbuf.at[v, :, zcol] for v in (0, 1)]

    def project(v):
        def use(rws, out):
            z = out.astype(BF16)
            hbuf[v, rws, zcol] = z
            zf = z.astype(F32)
            if not v:
                return zf,
            diff = zb[0][rws, :].astype(F32) - zf
            return zf, diff * diff

        for o, term in enumerate(by_rows(x2.at[v], w3b, use, 1 + v)):
            zs_src[0, one(v + o), :] = term

    def gram_of(v, chunk):
        if not chunk:
            for i in range(dim // BLK):
                zi = hbuf[v, :, span(i, dim)]
                sq = dot(zi, zi, TN)
                for row, lane, r, c, size, _ in PIECES[3 * i:3 * i + 3]:
                    gram[v, row:row + size, lane:lane + size] = sq[r - i * BLK:r - i * BLK + size, c - i * BLK:c - i * BLK + size]
        lo, hi = SPANS[chunk]
        for b, (i, j) in enumerate(OFF_PAIRS):
            row = TRI_ROWS + b * BLK
            if lo <= row < hi:
                gram[v, row:row + BLK, :] = dot(hbuf[v, :, span(i, dim)], hbuf[v, :, span(j, dim)], TN)
        reds[v][chunk].begin()

    reds = []
    for v in (0, 1):
        pair = []
        for ch, (lo, hi) in enumerate(SPANS):
            rws = pl.ds(lo, hi - lo)
            pair.append(GramReduce(place, gram.at[v, rws], ghat.at[v, rws], rc.at[v, ch], r1.at[v, ch], r2.at[v, ch],
                                   rd_ss.at[v, ch], rd_rs.at[v, ch]))
        reds.append(pair)
    (a0, a1), (b0, b1) = reds

    def store_outer(mus):
        for v in (0, 1):
            for row, lane, r, c, size, _ in PIECES:
                col = jnp.transpose(jnp.broadcast_to(mus[v][:, r:r + size], (size, size)))
                mu_outer[v, row:row + size, lane:lane + size] = (all_rows * col) * mus[v][:, c:c + size]

    def finish(v, ch):
        def fin(row, acc):
            leaf = acc.shape[0]
            row = SPANS[ch][0] + row
            prow = row + lax.broadcasted_iota(jnp.int32, acc.shape, 0)
            lane = lax.broadcasted_iota(jnp.int32, acc.shape, 1)
            quad = (prow < TRI_ROWS) & ((prow >= DIAG_ROWS) | (lane < QUAD))
            eye = quad & (lax.rem(prow, QUAD) == lax.rem(lane, QUAD))
            cov = (acc - mu_outer[v, pl.ds(pl.multiple_of(row, 16), leaf), :]) / (all_rows - 1)
            std = jnp.sqrt(cov + STD_EPS)
            hinge = jnp.where(eye, jnp.maximum(1.0 - std, 0.0), 0.0)
            off = jnp.where(eye, 0.0, cov * cov) * jnp.where(quad, 1.0, 2.0)
            term = col_sum(hinge + 2.0 * off)
            ls_src[0] = ls_src[0] + term[:, :LANES] + term[:, LANES:]
            on = jnp.where(std < 1.0, 1.0, 0.0)
            return jnp.where(eye, -on / (2.0 * std), 4.0 * cov).astype(BF16)
        return fin

    def expand(v):
        for row, lane, r, c, size, mirrored in PIECES:
            blk = ghat[v, row:row + size, lane:lane + size]
            w1b[v * dim + r:v * dim + r + size, c:c + size] = blk
            if mirrored:
                w1b[v * dim + c:v * dim + c + size, r:r + size] = jnp.transpose(blk)

    def grad_z(v, mu, between):
        hi = mu.astype(BF16)
        mid = (mu - hi.astype(F32)).astype(BF16)
        low = (mu - hi.astype(F32) - mid.astype(F32)).astype(BF16)
        parts = jnp.concatenate([hi, mid, low, jnp.zeros((13, dim), BF16)], axis=0)
        g = w1b.at[pl.ds(v * dim, dim)]
        mean_part = col_sum(dot(parts, g[...]))
        sign = -1.0 if v else 1.0

        for part in range(rows // ROWS):
            sub = pl.ds(part * ROWS, ROWS)
            za, zo, out = zb[0].at[sub], zb[1].at[sub], hbuf.at[v, sub, dzcol]

            def use(rws, row_part):
                diff = za[rws, :].astype(F32) - zo[rws, :].astype(F32)
                dz = (2.0 / (all_rows - 1)) * (row_part - mean_part) + (sign * 4.0 / all_rows) * diff
                out[rws, :] = dz.astype(BF16)
                return ()

            by_rows(zb[v].at[sub], g, use)
            put(out, dz_o.at[v, sub])
            if between:
                between.pop(0)()

    loads['w1'].wait()
    loads['ha'].wait()
    linear(0, u1.at[0], hbuf.at[0], w1b)
    loads['hb'].wait()
    linear(1, u1.at[1], hbuf.at[1], w1b)
    loads['w2'].wait()
    loads['w3'].wait()
    for v in (0, 1):
        norm_relu(v, v, 0, u1, x1)
        put(u1.at[v], n1_o.at[v])
        put(x1.at[v], x1_o.at[v])
        linear(2 + v, u2.at[v], x1.at[v], w2b)
    zs_src[0] = jnp.zeros(zs_src.shape[1:], F32)
    ls_src[0] = jnp.zeros((1, LANES), F32)
    norm_relu(2, 0, 1, u2, x2)
    put(u2.at[0], n2_o.at[0])
    put(x2.at[0], x2_o.at[0])
    project(0)
    gram_of(0, 0)
    gram_of(0, 1)
    norm_relu(3, 1, 1, u2, x2)
    put(u2.at[1], n2_o.at[1])
    put(x2.at[1], x2_o.at[1])
    a0.step_1()
    a1.step_1()
    project(1)
    zstats.send(0)
    gram_of(1, 0)
    gram_of(1, 1)
    a0.step_2()
    ztot = zstats.total(0)
    mus = [ztot[one(v)] / all_rows for v in (0, 1)]
    sq_sum = jnp.sum(ztot[one(2)])
    b0.step_1()
    a1.step_2()
    b1.step_1()
    store_outer(mus)
    a0.step_3(finish(0, 0))
    a1.step_3(finish(0, 1))
    a0.step_4()
    b0.step_2()
    a1.step_4()
    b1.step_2()
    b0.step_3(finish(1, 0))
    a0.step_5()
    b1.step_3(finish(1, 1))
    lstats.send(0)
    a1.step_5()
    b0.step_4()
    b1.step_4()
    a0.step_6()
    a1.step_6()
    expand(0)
    grad_z(0, mus[0], [b0.step_5])
    b1.step_5()
    b0.step_6()
    b1.step_6()
    expand(1)
    grad_z(1, mus[1], [])
    loss_o[...] = jnp.broadcast_to(jnp.sum(lstats.total(0)) + 2.0 * sq_sum / all_rows, loss_o.shape)
    for ex in (stats, zstats, lstats):
        ex.drain()
    for red in (a0, a1, b0, b1):
        red.drain()
    for cp in outs:
        cp.wait()


def forward(n_dev, h_a, h_b, w1, w2, w3, *affine):
    rows, feat = h_a.shape
    dim = w2.shape[0]
    all_rows = rows * n_dev
    half = max(hi - lo for lo, hi in SPANS)
    any_spec = pl.BlockSpec(memory_space=pl.ANY)
    vm = pl.BlockSpec(memory_space=pltpu.VMEM)
    wide = lambda dt: jax.ShapeDtypeStruct((2, rows, dim), dt)
    dma = pltpu.SemaphoreType.DMA
    return pl.pallas_call(
        functools.partial(fwd_kernel, all_rows),
        name='forward',
        out_shape=[wide(F32), wide(BF16), wide(F32), wide(BF16), wide(BF16),
                   jax.ShapeDtypeStruct((4, dim), F32), jax.ShapeDtypeStruct((1, LANES), F32)],
        in_specs=[any_spec] * 5 + [vm] * 4,
        out_specs=[any_spec] * 5 + [vm, vm],
        scratch_shapes=[
            pltpu.VMEM((2, rows, feat), BF16), pltpu.VMEM((feat, dim), BF16), pltpu.VMEM((dim, dim), BF16), pltpu.VMEM((dim, dim), BF16),
            pltpu.VMEM((2, rows, dim), F32), pltpu.VMEM((2, rows, dim), BF16), pltpu.VMEM((2, rows, dim), F32), pltpu.VMEM((2, rows, dim), BF16),
            pltpu.VMEM((2, PACKED, BLK), F32), pltpu.VMEM((2, PACKED, BLK), BF16), pltpu.VMEM((2, PACKED, BLK), F32),
            pltpu.VMEM((2, 2, half // 2, BLK), F32), pltpu.VMEM((2, 2, 2, half // 8, BLK), F32), pltpu.VMEM((2, 2, 2, half // 16, BLK), F32),
            pltpu.VMEM((4, 2, dim), F32), pltpu.VMEM((4, NDEV, 2, dim), F32),
            pltpu.VMEM((1, 4, dim), F32), pltpu.VMEM((1, NDEV, 4, dim), F32),
            pltpu.VMEM((1, 1, LANES), F32), pltpu.VMEM((1, NDEV, 1, LANES), F32),
            dma((5,)), dma((12,)), dma((4, NDEV)), dma((4, NDEV)), dma((1, NDEV)), dma((1, NDEV)), dma((1, NDEV)), dma((1, NDEV)),
            dma((2, 2, 10)), dma((2, 2, 10))],
        compiler_params=pltpu.CompilerParams(collective_id=0, has_side_effects=True, vmem_limit_bytes=VMEM_BYTES),
    )(h_a, h_b, w1, w2, w3, *affine)


CHUNK = 256
PART_SLOTS = 4
LAST_STEP = 6


class Chunks:
    def __init__(self, place, count, part, rc, r1, r2, out, ssem, rsem):
        self.place, self.count = place, count
        self.part, self.rc, self.r1, self.r2, self.out = part, rc, r1, r2, out
        self.ssem, self.rsem = ssem, rsem

    def reduce(self, t):
        ps = lax.rem(t, PART_SLOTS)
        return Reduce(self.place, self.part.at[ps], self.out.at[tile(t, CHUNK)], self.rc.at[ps], self.r1.at[ps], self.r2.at[ps],
                      self.ssem.at[t], self.rsem.at[t])

    def step(self, k, t):
        red = self.reduce(t)
        if k == 3:
            red.step_3(lambda row, acc: acc)
            for cp in red.cp_c() + red.cp_1() + red.cp_2():
                cp.wait_send()
        else:
            getattr(red, 'step_%d' % k)()
        if k == LAST_STEP:
            for cp in red.cp_g2() + red.cp_g1() + red.cp_gc():
                cp.wait_send()

    def steps(self, t):
        for k in range(1, LAST_STEP + 1):
            if not isinstance(t, int) or 0 <= t - k < self.count:
                self.step(k, t - k)


def bwd_kernel(all_rows, dz, x2, n2, w3, x1, n1, w2, h_a, h_b, inv, g1, b1, g2, b2,
               out, bn_o,
               dzb, x2b, x1b, nb, dxb, dub, w2b, w3b, part, rc, r1, r2, st_src, st_rcv,
               ld_sem, n_sem, h_sem, st_ss, st_rs, rd_ss, rd_rs):
    dim = w2b.shape[0]
    rows = h_a.shape[0]
    feat = h_a.shape[1]
    affine = ((g1, b1), (g2, b2))
    place = Place()
    view = [slice(0, rows), slice(rows, 2 * rows)]
    lanes = lambda j: slice(j * CHUNK, (j + 1) * CHUNK)
    per = dim // CHUNK
    pairs = [('dz', dz, dzb)] + [('x2%d' % j, x2.at[:, lanes(j)], x2b.at[:, lanes(j)]) for j in range(per)]
    pairs += [('w3', w3, w3b)] + [('n2%d' % v, n2.at[view[v]], nb.at[view[v]]) for v in (0, 1)] + [('w2', w2, w2b), ('x1', x1, x1b)]
    loads = {}
    for i, (name, src, dst) in enumerate(pairs):
        loads[name] = pltpu.make_async_copy(src, dst, ld_sem.at[i])
        loads[name].start()
    load_n1 = [pltpu.make_async_copy(n1.at[view[v]], nb.at[view[v]], n_sem.at[v]) for v in (0, 1)]

    first_one = 2 * (dim // CHUNK)
    count = first_one + feat // CHUNK

    def load_h(t):
        slot = lax.rem(t, 2)
        cols = tile(t - first_one, CHUNK)
        return [pltpu.make_async_copy(h.at[:, cols], x2b.at[view[v], tile(slot, CHUNK)], h_sem.at[slot, v]) for v, h in enumerate((h_a, h_b))]

    entry_barrier(place)
    stats = StatExchange(place, st_src, st_rcv, st_ss, st_rs)
    chunks = Chunks(place, count, part, rc, r1, r2, out, rd_ss, rd_rs)

    def weight_grad(t, lhs, rhs):
        part[lax.rem(t, PART_SLOTS)] = dot(lhs, rhs, TN)
        chunks.reduce(t).begin()

    def grad_act(slot, v, layer, src, w):
        gain, bias = affine[layer]
        n_ref, dst = nb.at[view[v]], dxb.at[view[v]]

        def use(rws, dx):
            n = n_ref[rws, :]
            da = jnp.where(gain[...] * n + bias[...] > 0.0, dx, 0.0)
            dst[rws, :] = da
            return da, da * n

        st_src[slot, ROW0, :], st_src[slot, ROW1, :] = by_rows(src.at[view[v]], w, use, 2, NT)
        stats.send(slot)

    def grad_pre(slot, v, layer, dst):
        sums = stats.total(slot)
        for row, o in ((ROW1, 2 * layer), (ROW0, 2 * layer + 1)):
            bn_o[one(o), :] = bn_o[one(o), :] + sums[row] if v else sums[row]
        mean_d = sums[ROW0] / all_rows
        mean_dn = sums[ROW1] / all_rows
        scale = inv[one(2 * layer + v), :] * affine[layer][0][...]

        def body(i):
            rws = tile(i, STRIP, v * rows)
            dst[rws, :] = (scale * (dxb[rws, :] - mean_d - nb[rws, :] * mean_dn)).astype(BF16)

        loop(rows // STRIP, body)

    loads['dz'].wait()
    for t in range(first_one):
        chunks.steps(t)
        j = t % per
        if t == per:
            grad_pre(0, 0, 1, dub)
            load_n1[0].start()
            grad_pre(1, 1, 1, dub)
            load_n1[1].start()
            loads['x1'].wait()
            loads['w2'].wait()
        if t < per:
            loads['x2%d' % j].wait()
            weight_grad(t, x2b[:, lanes(j)], dzb[...])
        else:
            weight_grad(t, x1b[:, lanes(j)], dub[...])
        if t == per - 2:
            loads['w3'].wait()
            loads['n20'].wait()
            grad_act(0, 0, 1, dzb, w3b)
        if t == per - 1:
            loads['n21'].wait()
            grad_act(1, 1, 1, dzb, w3b)
        if t == per:
            load_n1[0].wait()
            grad_act(2, 0, 0, dub, w2b)
        if t == per + 1:
            load_n1[1].wait()
            grad_act(3, 1, 0, dub, w2b)
        if t == per + 2:
            grad_pre(2, 0, 0, dzb)
        if t == per + 3:
            grad_pre(3, 1, 0, dzb)
            for cp in load_h(first_one):
                cp.start()

    def tick(t, _):
        chunks.steps(t)
        for cp in load_h(t):
            cp.wait()

        @pl.when(t + 1 < count)
        def _():
            for cp in load_h(t + 1):
                cp.start()

        weight_grad(t, x2b[:, tile(lax.rem(t, 2), CHUNK)], dzb[...])
        return 0

    lax.fori_loop(first_one, count, tick, 0)
    for t in range(count, count + LAST_STEP):
        chunks.steps(t)
    stats.drain()


def backward(n_dev, dz, x2, n2, w3, x1, n1, w2, h_a, h_b, inv, *affine):
    rows, feat = h_a.shape
    dim = w2.shape[0]
    all_rows = rows * n_dev
    flat = lambda a: a.reshape(2 * rows, dim)
    any_spec = pl.BlockSpec(memory_space=pl.ANY)
    vm = pl.BlockSpec(memory_space=pltpu.VMEM)
    dma = pltpu.SemaphoreType.DMA
    count = (2 * dim + feat) // CHUNK
    big = (2 * rows, dim)
    grad_bytes = (2 * dim + feat) * dim * 4
    return pl.pallas_call(
        functools.partial(bwd_kernel, all_rows),
        name='backward',
        out_shape=[pltpu.VMEM((2 * dim + feat, dim), F32), pltpu.VMEM((4, dim), F32)],
        in_specs=[any_spec] * 9 + [vm] * 5,
        out_specs=[vm, vm],
        scratch_shapes=[
            pltpu.VMEM(big, BF16), pltpu.VMEM(big, BF16), pltpu.VMEM(big, BF16), pltpu.VMEM(big, F32), pltpu.VMEM(big, F32), pltpu.VMEM(big, BF16),
            pltpu.VMEM((dim, dim), BF16), pltpu.VMEM((dim, dim), BF16), pltpu.VMEM((PART_SLOTS, CHUNK, dim), F32),
            pltpu.VMEM((PART_SLOTS, CHUNK // 2, dim), F32), pltpu.VMEM((PART_SLOTS, 2, CHUNK // 8, dim), F32),
            pltpu.VMEM((PART_SLOTS, 2, CHUNK // 16, dim), F32),
            pltpu.VMEM((4, 2, dim), F32), pltpu.VMEM((4, NDEV, 2, dim), F32),
            dma((10,)), dma((2,)), dma((2, 2)), dma((4, NDEV)), dma((4, NDEV)), dma((count, 10)), dma((count, 10))],
        compiler_params=pltpu.CompilerParams(collective_id=1, has_side_effects=True, vmem_limit_bytes=VMEM_BYTES - grad_bytes - SPARE),
    )(flat(dz), flat(x2), flat(n2), w3, flat(x1), flat(n1), w2, h_a, h_b, inv, *affine)


def emit_kernel(rows, grads, bn, loss, *refs):
    big, small, (sem,) = refs[:3], refs[3:8], refs[8:]
    copies = [pltpu.make_async_copy(grads.at[pl.ds(lo, hi - lo)], dst, sem.at[i]) for i, (dst, (lo, hi)) in enumerate(zip(big, rows))]
    for cp in copies:
        cp.start()
    for i in range(4):
        small[i][...] = bn[one(i), :]
    small[4][...] = loss[...]
    for cp in copies:
        cp.wait()


def emit(grads, bn, loss, dim):
    total = grads.shape[0]
    rows = ((2 * dim, total), (dim, 2 * dim), (0, dim))
    any_spec = pl.BlockSpec(memory_space=pl.ANY)
    vm = pl.BlockSpec(memory_space=pltpu.VMEM)
    vec = jax.ShapeDtypeStruct((1, dim), F32)
    return pl.pallas_call(
        functools.partial(emit_kernel, rows),
        name='emit',
        out_shape=[jax.ShapeDtypeStruct((hi - lo, dim), F32) for lo, hi in rows] + [vec] * 4 + [jax.ShapeDtypeStruct((1, LANES), F32)],
        in_specs=[vm, vm, vm],
        out_specs=[any_spec] * 3 + [vm] * 5,
        scratch_shapes=[pltpu.SemaphoreType.DMA((3,))],
        compiler_params=pltpu.CompilerParams(vmem_limit_bytes=VMEM_BYTES // 16),
    )(pltpu.with_memory_space_constraint(grads, pltpu.VMEM), bn, loss)


def solution(mesh):
    n_dev = mesh.shape['data']

    def local_step(h_a, h_b, w_one, w_two, w_three, gain_one, bias_one, gain_two, bias_two):
        affine = [v.reshape(1, -1) for v in (gain_one, bias_one, gain_two, bias_two)]
        norm1, x1, norm2, x2, d_z, inv, loss = forward(n_dev, h_a, h_b, w_one, w_two, w_three, *affine)
        grads, bn = backward(n_dev, d_z, x2, norm2, w_three, x1, norm1, w_two, h_a, h_b, inv, *affine)
        d_one, d_two, d_three, *small, loss = emit(grads, bn, loss, w_two.shape[0])
        return (loss[0, 0], d_one, d_two, d_three) + tuple(v.reshape(-1) for v in small)

    row = P('data', None)
    return jax.shard_map(local_step, mesh=mesh, in_specs=(row, row) + (P(),) * 7, out_specs=(P(),) * 8, check_vma=False)
```

time: 432 us -> 233 us (0.54)
  waiting for transfers between devices: 207 us -> 0 us
  Pallas kernels: 82.4 us -> 232 us
  matrix products: 46.4 us -> 0 us
  blocking collectives: 45.7 us -> 0 us
  other arithmetic: 17.9 us -> 0 us
  local copies, waits for them, and re-layouts: 17.4 us -> 0.01 us
  between operations: 14.2 us -> 0.84 us
    psum x1 -> x0, waiting for transfers between devices: 207 us -> none  [local_step(): lax.psum((grad_one, grad_two, grad_three), 'data')]
    pallas_call x0 -> x2, Pallas kernels: none -> 160 us  [the longest x1 153 us: backward(): pl.pallas_call(functools.partial(bwd_kernel, all_rows), name='backward',...]
    dot_general x6 -> x0, matrix products: 46.4 us -> none  [the longest x1 10.2 us: local_step(): d_x1 = jnp.einsum('vnd,kd->vnk', d_u2, w_two, preferred_element_type=F32)]
    psum x2 -> x0, blocking collectives: 45.7 us -> none  [layer_backward(): lax.psum(jnp.stack([jnp.sum(d_act, axis=1), jnp.sum(d_act * normed, axis=...]
    unnamed x27 -> x2, local copies, waits for them, and re-layouts: 16.3 us -> 0.01 us
    convert_element_type x2 -> x0, other arithmetic: 14.4 us -> none  [layer_backward(): d_pre.astype(BF16)]
    pallas_call x1, Pallas kernels: 82.4 us -> 72.7 us  [forward(): pl.pallas_call(functools.partial(fwd_kernel, all_rows), name='forward', o...]
  transfers between devices with their start and end apart: 1 -> 0, of which waited for: 1 -> 0; matrix products, arithmetic and copies ran while one was open for 0% -> 0% of each run, Pallas kernels for 0% -> 0%
where the time goes in v2:
time: 233 us
  Pallas kernels  232 us (100%)
    pallas_call x1, Pallas kernels, backward(): pl.pallas_call(functools.partial(bwd_kernel, all_rows), name='backward',...  153 us
    pallas_call x1, Pallas kernels, forward(): pl.pallas_call(functools.partial(fwd_kernel, all_rows), name='forward', o...  72.7 us
    pallas_call x1, Pallas kernels, emit(): pl.pallas_call(functools.partial(emit_kernel, rows), name='emit', out_sha...  6.67 us

profile of v2, /device:TPU:0, one launch (start us, length us, event | category | flops | bytes accessed | tf_op | source)
XLA Modules:
  0.0 233.3 jit_solution(4372354346848481935)
XLA Ops:
  0.6 72.7 %forward.1 = (f32[2,1024,1024]{2,1,0:T(8,128)}, bf16[2,1024,1024]{2,1,0:T(8,128)(2,1)}, f32[2,1024,1024]{2,1,0:T(8,128)}, bf16[2,1024,1024]{2,1,0:T(8,128)(2,1)}...) custom-call(bf16[1024,2048]{1,0:T(8,128)(2,1)} %h_a.3, bf16[1024,2048]{1,0:T(8,128)(2,1)} %h_b.3, ...), custom_call_target="tpu_custom_call" | custom-call | tf_op jit(solution)/shard_map/forward/pallas_call | solution.py:467
  73.3 0.0 copy-start
  73.3 153.1 %backward.1 = (f32[4096,1024]{1,0:T(8,128)S(1)}, f32[4,1024]{1,0:T(4,128)S(1)}) custom-call(bf16[2048,1024]{1,0:T(8,128)(2,1)} %bitcast.19, bf16[2048,1024]{1,0:T(8,128)(2,1)} %bitcast.18, f32[2048,1024]{1,0:T(8,128)} %bitcast.16, bf16[1024,1024]{1,0:T(8,128)(2,1)} %w3.3, bf16[2048,1024]{1,0:T(8,128)(2,1)} %bitcast.17, f32[2048,1024]{1,0:T(8,128)} %bitcast.15, ...), custom_call_target="tpu_custom_call" | custom-call | tf_op jit(solution)/shard_map/backward/pallas_call | solution.py:651
  226.4 0.0 copy-done
  226.4 6.7 %emit.1 = (f32[2048,1024]{1,0:T(8,128)}, f32[1024,1024]{1,0:T(8,128)}, f32[1024,1024]{1,0:T(8,128)}, f32[1,1024]{1,0:T(1,128)}, f32[1,1024]{1,0:T(1,128)}, /*ind...) custom-call(f32[4096,1024]{1,0:T(8,128)S(1)} %get-tuple-element.31.grads, f32[4,1024]{1,0:T(4,128)S(1)} %get-tuple-element.32.bn, ...), custom_call_target="tpu_custom_call" | custom-call | tf_op jit(solution)/shard_map/emit/pallas_call | solution.py:686
Async XLA Ops:
  73.3 153.1 %copy-start = (f32[1,128]{1,0:T(1,128)S(1)}, f32[1,128]{1,0:T(1,128)}, u32[]{:S(2)}) copy-start(f32[1,128]{1,0:T(1,128)} %get-tuple-element.33.loss) | copy-start | bytes 1540

commit v3 on v2

v3 whole, which is shorter than its diff:
```python
import functools

import jax
import jax.numpy as jnp
from jax import lax
from jax.experimental import pallas as pl
from jax.experimental.pallas import tpu as pltpu
from jax.sharding import PartitionSpec as P

BN_EPS = 1e-5
STD_EPS = 1e-4
F32 = jnp.float32
BF16 = jnp.bfloat16
MESH = pl.DeviceIdType.MESH
NDEV = 8
BLK = 256
STRIP = 64
SPARE = 524288
ROWS = 512
VMEM_BYTES = 67043328
LANES = 128
QUAD = 128
DIAG_ROWS = 4 * QUAD
TRI_ROWS = 6 * QUAD
OFF_PAIRS = [(0, 1), (0, 2), (0, 3), (1, 2), (1, 3), (2, 3)]
PIECES = []
for _i in range(4):
    _b = _i * BLK
    PIECES += [(_i * QUAD, 0, _b, _b, QUAD, False), (_i * QUAD, QUAD, _b, _b + QUAD, QUAD, True),
               (DIAG_ROWS + _i // 2 * QUAD, _i % 2 * QUAD, _b + QUAD, _b + QUAD, QUAD, False)]
PIECES += [(TRI_ROWS + _b * BLK, 0, _i * BLK, _j * BLK, BLK, True) for _b, (_i, _j) in enumerate(OFF_PAIRS)]
PACKED = TRI_ROWS + len(OFF_PAIRS) * BLK
SPLIT = TRI_ROWS + 2 * BLK
SPANS = ((0, SPLIT), (SPLIT, PACKED))
ROW0, ROW1 = slice(0, 1), slice(1, 2)
TN = (((0,), (0,)), ((), ()))
NT = (((1,), (1,)), ((), ()))


def dot(a, b, dims=(((1,), (0,)), ((), ()))):
    return lax.dot_general(a, b, dims, preferred_element_type=F32)


def col_sum(v):
    return jnp.sum(v, axis=0, keepdims=True)


def one(i):
    return slice(i, i + 1)


def tile(j, size=BLK, base=0):
    return pl.ds(pl.multiple_of(base + j * size, size), size)


def span(i, base=0):
    return slice(base + i * BLK, base + i * BLK + BLK)


def loop(count, body):
    def step(i, carry):
        body(i)
        return carry

    lax.fori_loop(0, count, step, 0)


class Place:
    def __init__(self):
        me = lax.axis_index('data')
        self.me = me
        self.c = lax.rem(me, 2)
        self.x = lax.rem(me // 2, 2)
        self.y = me // 4

    def flip(self, dy, dx, dc):
        y = 1 - self.y if dy else self.y
        x = 1 - self.x if dx else self.x
        c = 1 - self.c if dc else self.c
        return y * 4 + x * 2 + c

    def peer(self, o):
        return self.flip(o & 4, o & 2, o & 1)


def entry_barrier(place):
    barrier = pltpu.get_barrier_semaphore()
    for o in range(1, NDEV):
        pl.semaphore_signal(barrier, inc=1, device_id=(place.peer(o),), device_id_type=MESH)
    pl.semaphore_wait(barrier, NDEV - 1)


class StatExchange:
    def __init__(self, place, src, rcv, ssem, rsem):
        self.place, self.src, self.rcv, self.ssem, self.rsem = place, src, rcv, ssem, rsem
        self.sent = []

    def copies(self, slot):
        place = self.place
        return [pltpu.make_async_remote_copy(
            src_ref=self.src.at[slot], dst_ref=self.rcv.at[slot, place.me],
            send_sem=self.ssem.at[slot, o], recv_sem=self.rsem.at[slot, o],
            device_id=(place.peer(o),), device_id_type=MESH) for o in range(1, NDEV)]

    def send(self, slot):
        self.rcv[slot, self.place.me] = self.src[slot]
        for cp in self.copies(slot):
            cp.start()
        self.sent.append(slot)

    def total(self, slot):
        for cp in self.copies(slot):
            cp.wait_recv()
        acc = self.rcv[slot, 0]
        for d in range(1, NDEV):
            acc = acc + self.rcv[slot, d]
        return acc

    def drain(self):
        for slot in self.sent:
            for cp in self.copies(slot):
                cp.wait_send()


class Reduce:
    def __init__(self, place, part, full, rc, r1, r2, ssem, rsem):
        self.place, self.part, self.full = place, part, full
        self.ssem, self.rsem = ssem, rsem
        self.rows = part.shape[0]
        self.rc, self.r1, self.r2 = rc, r1, r2
        place_pq = [(place.x, place.y), (place.y, place.x)]
        rows, c = self.rows, place.c
        al = rows // 16
        self.leaf_rows = al
        mo = lambda v: pl.multiple_of(v, al)
        self.half_mine = mo(c * (rows // 2))
        self.half_other = mo((1 - c) * (rows // 2))
        self.o1_mine, self.o1_other, self.o2_mine, self.o2_other = [], [], [], []
        for k, (p, q) in enumerate(place_pq):
            base = c * (rows // 2) + k * (rows // 4)
            self.o1_mine.append(mo(base + p * (rows // 8)))
            self.o1_other.append(mo(base + (1 - p) * (rows // 8)))
            self.o2_mine.append(mo(base + p * (rows // 8) + q * (rows // 16)))
            self.o2_other.append(mo(base + p * (rows // 8) + (1 - q) * (rows // 16)))
        self.dev_c = place.flip(0, 0, 1)
        self.dev_1 = [place.flip(0, 1, 0), place.flip(1, 0, 0)]
        self.dev_2 = [place.flip(1, 0, 0), place.flip(0, 1, 0)]

    def _cp(self, idx, src, dst, dev):
        return pltpu.make_async_remote_copy(src_ref=src, dst_ref=dst, send_sem=self.ssem.at[idx], recv_sem=self.rsem.at[idx],
                                            device_id=(dev,), device_id_type=MESH)

    def cp_c(self):
        return [self._cp(0, self.part.at[pl.ds(self.half_other, self.rows // 2)], self.rc, self.dev_c)]

    def cp_1(self):
        return [self._cp(1 + k, self.part.at[pl.ds(self.o1_other[k], self.rows // 8)], self.r1[k], self.dev_1[k]) for k in (0, 1)]

    def cp_2(self):
        return [self._cp(3 + k, self.part.at[pl.ds(self.o2_other[k], self.rows // 16)], self.r2[k], self.dev_2[k]) for k in (0, 1)]

    def cp_g2(self):
        return [self._cp(5 + k, self.full.at[pl.ds(self.o2_mine[k], self.rows // 16)],
                         self.full.at[pl.ds(self.o2_mine[k], self.rows // 16)], self.dev_2[k]) for k in (0, 1)]

    def cp_g1(self):
        return [self._cp(7 + k, self.full.at[pl.ds(self.o1_mine[k], self.rows // 8)],
                         self.full.at[pl.ds(self.o1_mine[k], self.rows // 8)], self.dev_1[k]) for k in (0, 1)]

    def cp_gc(self):
        half = pl.ds(self.half_mine, self.rows // 2)
        return [self._cp(9, self.full.at[half], self.full.at[half], self.dev_c)]

    @staticmethod
    def start(cps):
        for cp in cps:
            cp.start()

    def begin(self):
        self.start(self.cp_c())

    def step_1(self):
        self.cp_c()[0].wait_recv()
        mine = pl.ds(self.half_mine, self.rows // 2)
        self.part[mine] = self.part[mine] + self.rc[...]
        self.start(self.cp_1())

    def step_2(self):
        for k, (cp, nxt) in enumerate(zip(self.cp_1(), self.cp_2())):
            cp.wait_recv()
            mine = pl.ds(self.o1_mine[k], self.rows // 8)
            self.part[mine] = self.part[mine] + self.r1[k][...]
            nxt.start()

    def step_3(self, finish):
        for k, (cp, nxt) in enumerate(zip(self.cp_2(), self.cp_g2())):
            cp.wait_recv()
            mine = pl.ds(self.o2_mine[k], self.rows // 16)
            self.full[mine] = finish(self.o2_mine[k], self.part[mine] + self.r2[k][...])
            nxt.start()

    def step_4(self):
        for cp in self.cp_g2():
            cp.wait_recv()
        self.start(self.cp_g1())

    def step_5(self):
        for cp in self.cp_g1():
            cp.wait_recv()
        self.start(self.cp_gc())

    def step_6(self):
        self.cp_gc()[0].wait_recv()

    def drain_part(self):
        for cp in self.cp_c() + self.cp_1() + self.cp_2():
            cp.wait_send()

    def drain_full(self):
        for cp in self.cp_g2() + self.cp_g1() + self.cp_gc():
            cp.wait_send()


def by_rows(lhs, rhs, use, sums=0, dims=(((1,), (0,)), ((), ()))):
    def step(i, carry):
        rws = tile(i, ROWS)
        terms = use(rws, dot(lhs[rws, :], rhs[...], dims))
        return tuple(c + col_sum(t) for c, t in zip(carry, terms))

    width = rhs.shape[1 - dims[0][1][0]]
    return lax.fori_loop(0, lhs.shape[0] // ROWS, step, (jnp.zeros((1, width), F32),) * sums)


CHUNK, SMALL = 256, 128
LEAD, EVEN, TAIL = 0, 16, 0
COUNT = LEAD + EVEN + TAIL
PART_SLOTS, CORE_SLOTS, LINK_SLOTS = 3, 2, 4
LAST_STEP = 6


def chunk_of(t):
    if not isinstance(t, int) or LEAD <= t < LEAD + EVEN:
        return (t - LEAD) * CHUNK + LEAD * SMALL, CHUNK
    if t < LEAD:
        return t * SMALL, SMALL
    return EVEN * CHUNK + (t - EVEN) * SMALL, SMALL


class Chunks:
    def __init__(self, place, part, net, out, ssem, rsem):
        self.place, self.part, self.net, self.out = place, part, net, out
        self.ssem, self.rsem = ssem, rsem

    def reduce(self, t):
        row, size = chunk_of(t)
        link = lax.rem(t, LINK_SLOTS)

        def landing(base, slot, room, used):
            return self.net.at[pl.ds(pl.multiple_of(base + slot * room, 8), used)]

        one_base = CORE_SLOTS * CHUNK // 2
        two_base = one_base + LINK_SLOTS * CHUNK // 4
        return Reduce(self.place, self.part_of(t), self.out.at[pl.ds(pl.multiple_of(row, SMALL), size)],
                      landing(0, lax.rem(t, CORE_SLOTS), CHUNK // 2, size // 2),
                      [landing(one_base, 2 * link + k, CHUNK // 8, size // 8) for k in (0, 1)],
                      [landing(two_base, 2 * link + k, CHUNK // 16, size // 16) for k in (0, 1)], self.ssem.at[t], self.rsem.at[t])

    def part_of(self, t):
        return self.part.at[pl.ds(pl.multiple_of(lax.rem(t, PART_SLOTS) * CHUNK, CHUNK), chunk_of(t)[1])]

    def step(self, k, t):
        red = self.reduce(t)
        if k == 3:
            red.step_3(lambda row, acc: acc)
            red.drain_part()
        else:
            getattr(red, 'step_%d' % k)()
        if k == LAST_STEP:
            red.drain_full()

    def steps(self, t):
        for k in range(1, LAST_STEP + 1):
            if not isinstance(t, int) or 0 <= t - k < COUNT:
                self.step(k, t - k)


GramReduce = Reduce


def step_kernel(all_rows, h_a, h_b, w1, w2, w3, g1, b1, g2, b2,
                grads, bn_o, loss_o, n1_o,
                hbuf, w1b, w2b, w3b, x1, x2, nb, ghat, part, net, invs,
                st_src, st_rcv, zs_src, zs_rcv, ls_src, ls_rcv,
                ld_sem, n_sem, h_sem, st_ss, st_rs, zs_ss, zs_rs, ls_ss, ls_rs, gr_ss, gr_rs, rd_ss, rd_rs):
    dim = w2b.shape[0]
    rows, feat = h_a.shape
    affine = ((g1, b1), (g2, b2))
    view = [slice(0, rows), slice(rows, 2 * rows)]
    low, high = slice(0, 2 * dim), slice(2 * dim, 2 * dim + feat)
    u1, dxb = grads.at[low], grads.at[high]
    place = Place()
    h_all = (h_a, h_b)
    loads = {}
    for name, src, dst in (('w1', w1, w1b), ('ha', h_a, hbuf.at[view[0]]), ('hb', h_b, hbuf.at[view[1]]), ('w2', w2, w2b), ('w3', w3, w3b)):
        loads[name] = pltpu.make_async_copy(src, dst, ld_sem.at[len(loads)])
        loads[name].start()
    spill = [pltpu.make_async_copy(u1.at[view[v]], n1_o.at[view[v]], n_sem.at[v]) for v in (0, 1)]
    load_n1 = [pltpu.make_async_copy(n1_o.at[view[v]], nb.at[view[v]], n_sem.at[v]) for v in (0, 1)]

    def lanes(row, size):
        return pl.ds(pl.multiple_of(row, SMALL), size)

    entry_barrier(place)
    stats = StatExchange(place, st_src, st_rcv, st_ss, st_rs)
    zstats = StatExchange(place, zs_src, zs_rcv, zs_ss, zs_rs)
    lstats = StatExchange(place, ls_src, ls_rcv, ls_ss, ls_rs)

    def linear(slot, dst, lhs, rhs):
        def use(rws, out):
            dst[rws, :] = out
            return out, out * out

        st_src[slot, ROW0, :], st_src[slot, ROW1, :] = by_rows(lhs, rhs, use, 2)
        stats.send(slot)

    def norm_relu(slot, v, layer, ubuf, xbuf):
        mom = stats.total(slot)
        mean = mom[ROW0] / all_rows
        var = mom[ROW1] / all_rows - mean * mean
        inv = lax.rsqrt(var + BN_EPS)
        invs[one(slot), :] = inv
        gain, bias = affine[layer]

        def body(i):
            rws = tile(i, STRIP, v * rows)
            n = (ubuf[rws, :] - mean) * inv
            ubuf[rws, :] = n
            xbuf[rws, :] = jnp.maximum(gain[...] * n + bias[...], 0.0).astype(BF16)

        loop(rows // STRIP, body)

    zcol = pl.ds(dim, dim)
    dzb = hbuf.at[:, pl.ds(0, dim)]
    zb = [hbuf.at[view[v], zcol] for v in (0, 1)]

    def project(v):
        def use(rws, out):
            z = out.astype(BF16)
            zb[v][rws, :] = z
            zf = z.astype(F32)
            if not v:
                return zf,
            diff = zb[0][rws, :].astype(F32) - zf
            return zf, diff * diff

        for o, term in enumerate(by_rows(x2.at[view[v]], w3b, use, 1 + v)):
            zs_src[0, one(v + o), :] = term

    outer, gram = grads.at[low], grads.at[high]

    def band(v, ch):
        return pl.ds((2 * v + ch) * BLK, BLK)

    def packed_at(ref, v, row, lane, size):
        ch = int(row >= SPLIT)
        return ref.at[pl.ds(row - SPANS[ch][0], size), pl.ds((2 * v + ch) * BLK + lane, size)]

    gram_at = functools.partial(packed_at, gram)

    def gram_of(v, chunk):
        if not chunk:
            for i in range(dim // BLK):
                zi = hbuf[view[v], span(i, dim)]
                sq = dot(zi, zi, TN)
                for row, lane, r, c, size, _ in PIECES[3 * i:3 * i + 3]:
                    gram_at(v, row, lane, size)[...] = sq[r - i * BLK:r - i * BLK + size, c - i * BLK:c - i * BLK + size]
        lo, hi = SPANS[chunk]
        for b, (i, j) in enumerate(OFF_PAIRS):
            row = TRI_ROWS + b * BLK
            if lo <= row < hi:
                gram_at(v, row, 0, BLK)[...] = dot(hbuf[view[v], span(i, dim)], hbuf[view[v], span(j, dim)], TN)
        reds[v][chunk].begin()

    reds = []
    for v in (0, 1):
        pair = []
        for ch, (lo, hi) in enumerate(SPANS):
            n, bd = hi - lo, band(v, ch)
            r1 = [net.at[pl.ds(k * n // 8, n // 8), bd] for k in (0, 1)]
            r2 = [net.at[pl.ds(n // 4 + k * n // 16, n // 16), bd] for k in (0, 1)]
            pair.append(GramReduce(place, gram.at[pl.ds(0, n), bd], ghat.at[v, pl.ds(lo, n)], part.at[pl.ds(0, n // 2), bd], r1, r2,
                                   gr_ss.at[v, ch], gr_rs.at[v, ch]))
        reds.append(pair)
    (a0, a1), (b0, b1) = reds

    def store_outer(mus):
        for v in (0, 1):
            for row, lane, r, c, size, _ in PIECES:
                col = jnp.transpose(jnp.broadcast_to(mus[v][:, r:r + size], (size, size)))
                packed_at(outer, v, row, lane, size)[...] = (all_rows * col) * mus[v][:, c:c + size]

    def finish(v, ch):
        def fin(row, acc):
            leaf = acc.shape[0]
            prow = SPANS[ch][0] + row + lax.broadcasted_iota(jnp.int32, acc.shape, 0)
            lane = lax.broadcasted_iota(jnp.int32, acc.shape, 1)
            quad = (prow < TRI_ROWS) & ((prow >= DIAG_ROWS) | (lane < QUAD))
            eye = quad & (lax.rem(prow, QUAD) == lax.rem(lane, QUAD))
            cov = (acc - outer[pl.ds(row, leaf), band(v, ch)]) / (all_rows - 1)
            std = jnp.sqrt(cov + STD_EPS)
            hinge = jnp.where(eye, jnp.maximum(1.0 - std, 0.0), 0.0)
            off = jnp.where(eye, 0.0, cov * cov) * jnp.where(quad, 1.0, 2.0)
            term = col_sum(hinge + 2.0 * off)
            ls_src[0] = ls_src[0] + term[:, :LANES] + term[:, LANES:]
            on = jnp.where(std < 1.0, 1.0, 0.0)
            return jnp.where(eye, -on / (2.0 * std), 4.0 * cov).astype(BF16)
        return fin

    def expand(v):
        for row, lane, r, c, size, mirrored in PIECES:
            blk = ghat[v, row:row + size, lane:lane + size]
            w1b[v * dim + r:v * dim + r + size, c:c + size] = blk
            if mirrored:
                w1b[v * dim + c:v * dim + c + size, r:r + size] = jnp.transpose(blk)

    def grad_z(v, mu, between):
        hi = mu.astype(BF16)
        mid = (mu - hi.astype(F32)).astype(BF16)
        low = (mu - hi.astype(F32) - mid.astype(F32)).astype(BF16)
        parts = jnp.concatenate([hi, mid, low, jnp.zeros((13, dim), BF16)], axis=0)
        g = w1b.at[pl.ds(v * dim, dim)]
        mean_part = col_sum(dot(parts, g[...]))
        sign = -1.0 if v else 1.0

        for part in range(rows // ROWS):
            sub = pl.ds(part * ROWS, ROWS)
            za, zo, out = zb[0].at[sub], zb[1].at[sub], dzb.at[pl.ds(v * rows + part * ROWS, ROWS)]

            def use(rws, row_part):
                diff = za[rws, :].astype(F32) - zo[rws, :].astype(F32)
                dz = (2.0 / (all_rows - 1)) * (row_part - mean_part) + (sign * 4.0 / all_rows) * diff
                out[rws, :] = dz.astype(BF16)
                return ()

            by_rows(zb[v].at[sub], g, use)
            if between:
                between.pop(0)()

    chunks = Chunks(place, part, net, grads, rd_ss, rd_rs)

    def load_h(t):
        row, size = chunk_of(t)
        slot = lax.rem(t, 2)
        return [pltpu.make_async_copy(h.at[:, lanes(row - 2 * dim, size)], x2.at[view[v], lanes(slot * CHUNK, size)], h_sem.at[slot, v])
                for v, h in enumerate(h_all)]

    def weight_grad(t, lhs, rhs):
        dst = chunks.part_of(t)

        def half(j):
            cols = tile(j, ROWS)
            dst[:, cols] = dot(lhs[...], rhs[:, cols], TN)

        loop(dim // ROWS, half)
        chunks.reduce(t).begin()

    def grad_act(slot, v, layer, src, w):
        gain, bias = affine[layer]
        n_ref, dst = nb.at[view[v]], dxb.at[view[v]]

        def use(rws, dx):
            n = n_ref[rws, :]
            da = jnp.where(gain[...] * n + bias[...] > 0.0, dx, 0.0)
            dst[rws, :] = da
            return da, da * n

        st_src[slot, ROW0, :], st_src[slot, ROW1, :] = by_rows(src.at[view[v]], w, use, 2, NT)
        stats.send(slot)

    def grad_pre(slot, v, layer, dst):
        sums = stats.total(slot)
        for row, o in ((ROW1, 2 * layer), (ROW0, 2 * layer + 1)):
            bn_o[one(o), :] = bn_o[one(o), :] + sums[row] if v else sums[row]
        mean_d = sums[ROW0] / all_rows
        mean_dn = sums[ROW1] / all_rows
        scale = invs[one(2 * layer + v), :] * affine[layer][0][...]

        def body(i):
            rws = tile(i, STRIP, v * rows)
            dst[rws, :] = (scale * (dxb[rws, :] - mean_d - nb[rws, :] * mean_dn)).astype(BF16)

        loop(rows // STRIP, body)

    loads['w1'].wait()
    loads['ha'].wait()
    linear(0, u1.at[view[0]], hbuf.at[view[0]], w1b)
    loads['hb'].wait()
    linear(1, u1.at[view[1]], hbuf.at[view[1]], w1b)
    loads['w2'].wait()
    loads['w3'].wait()
    for v in (0, 1):
        norm_relu(v, v, 0, u1, x1)
        spill[v].start()
        linear(2 + v, nb.at[view[v]], x1.at[view[v]], w2b)
    zs_src[0] = jnp.zeros(zs_src.shape[1:], F32)
    ls_src[0] = jnp.zeros((1, LANES), F32)
    norm_relu(2, 0, 1, nb, x2)
    project(0)
    gram_of(0, 0)
    gram_of(0, 1)
    norm_relu(3, 1, 1, nb, x2)
    a0.step_1()
    a1.step_1()
    project(1)
    zstats.send(0)
    gram_of(1, 0)
    gram_of(1, 1)
    a0.step_2()
    ztot = zstats.total(0)
    mus = [ztot[one(v)] / all_rows for v in (0, 1)]
    sq_sum = jnp.sum(ztot[one(2)])
    b0.step_1()
    a1.step_2()
    b1.step_1()
    for cp in spill:
        cp.wait()
    store_outer(mus)
    a0.step_3(finish(0, 0))
    a1.step_3(finish(0, 1))
    a0.step_4()
    b0.step_2()
    a1.step_4()
    b1.step_2()
    b0.step_3(finish(1, 0))
    a0.step_5()
    b1.step_3(finish(1, 1))
    lstats.send(0)
    a1.step_5()
    b0.step_4()
    b1.step_4()
    a0.step_6()
    a1.step_6()
    expand(0)
    grad_z(0, mus[0], [b0.step_5])
    lead = lanes(0, chunk_of(0)[1])
    chunks.part_of(0)[...] = dot(x2[view[0], lead], dzb[view[0], :], TN)
    b1.step_5()
    b0.step_6()
    b1.step_6()
    expand(1)
    grad_z(1, mus[1], [])
    for red in (a0, a1, b0, b1):
        red.drain_part()

    dub, du1 = w1b, hbuf.at[:, zcol]
    first_two = next(t for t in range(COUNT) if chunk_of(t)[0] >= dim)
    first_one = next(t for t in range(COUNT) if chunk_of(t)[0] >= 2 * dim)
    extra = {
        first_two - 2: lambda: grad_act(4, 0, 1, dzb, w3b),
        first_two - 1: lambda: grad_act(5, 1, 1, dzb, w3b),
        first_two: lambda: (load_n1[0].wait(), grad_act(6, 0, 0, dub, w2b)),
        first_two + 1: lambda: (load_n1[1].wait(), grad_act(7, 1, 0, dub, w2b)),
        first_two + 2: lambda: grad_pre(6, 0, 0, du1),
        first_two + 3: lambda: (grad_pre(7, 1, 0, du1), [cp.start() for cp in load_h(first_one)]),
    }

    def weight_tick(t):
        for cp in load_h(t):
            cp.wait()
        if not isinstance(t, int) or t + 1 < COUNT:
            for cp in load_h(t + 1):
                cp.start()
        weight_grad(t, x2.at[:, lanes(lax.rem(t, 2) * CHUNK, chunk_of(t)[1])], du1)

    for t in range(first_one):
        chunks.steps(t)
        if t == first_two:
            for v in (0, 1):
                grad_pre(4 + v, v, 1, dub)
                load_n1[v].start()
        row, size = chunk_of(t)
        if not t:
            chunks.part_of(t)[...] = chunks.part_of(t)[...] + dot(x2[view[1], lead], dzb[view[1], :], TN)
            chunks.reduce(t).begin()
        elif t < first_two:
            weight_grad(t, x2.at[:, lanes(row, size)], dzb)
        else:
            weight_grad(t, x1.at[:, lanes(row - dim, size)], dub)
        if t in extra:
            extra[t]()

    def tick(t):
        chunks.steps(t)
        weight_tick(t)

    last_even = LEAD + EVEN - 1
    loop(last_even - first_one, lambda i: tick(first_one + i))
    for t in range(last_even, COUNT + LAST_STEP):
        chunks.steps(t)
        if t < COUNT:
            weight_tick(t)
    loss_o[...] = jnp.broadcast_to(jnp.sum(lstats.total(0)) + 2.0 * sq_sum / all_rows, loss_o.shape)
    for ex in (stats, zstats, lstats):
        ex.drain()
    for red in (a0, a1, b0, b1):
        red.drain_full()


def train_step(n_dev, h_a, h_b, w1, w2, w3, *affine):
    rows, feat = h_a.shape
    dim = w2.shape[0]
    total = 2 * dim + feat
    any_spec = pl.BlockSpec(memory_space=pl.ANY)
    vm = pl.BlockSpec(memory_space=pltpu.VMEM)
    dma = pltpu.SemaphoreType.DMA
    wide = (2 * rows, dim)
    moments = (2, dim)
    return pl.pallas_call(
        functools.partial(step_kernel, rows * n_dev),
        name='train_step',
        out_shape=[pltpu.VMEM((total, dim), F32), pltpu.VMEM((4, dim), F32), pltpu.VMEM((1, LANES), F32), jax.ShapeDtypeStruct(wide, F32)],
        in_specs=[any_spec] * 5 + [vm] * 4,
        out_specs=[vm] * 3 + [any_spec],
        scratch_shapes=[
            pltpu.VMEM((2 * rows, feat), BF16), pltpu.VMEM((feat, dim), BF16), pltpu.VMEM((dim, dim), BF16), pltpu.VMEM((dim, dim), BF16),
            pltpu.VMEM(wide, BF16), pltpu.VMEM(wide, BF16), pltpu.VMEM(wide, F32), pltpu.VMEM((2, PACKED, BLK), BF16),
            pltpu.VMEM((PART_SLOTS * CHUNK, dim), F32), pltpu.VMEM((CORE_SLOTS * CHUNK // 2 + LINK_SLOTS * CHUNK * 3 // 8, dim), F32),
            pltpu.VMEM((4, dim), F32),
            pltpu.VMEM((8,) + moments, F32), pltpu.VMEM((8, NDEV) + moments, F32),
            pltpu.VMEM((1, 4, dim), F32), pltpu.VMEM((1, NDEV, 4, dim), F32),
            pltpu.VMEM((1, 1, LANES), F32), pltpu.VMEM((1, NDEV, 1, LANES), F32),
            dma((5,)), dma((2,)), dma((2, 2)), dma((8, NDEV)), dma((8, NDEV)), dma((1, NDEV)), dma((1, NDEV)), dma((1, NDEV)), dma((1, NDEV)),
            dma((2, 2, 10)), dma((2, 2, 10)), dma((COUNT, 10)), dma((COUNT, 10))],
        compiler_params=pltpu.CompilerParams(collective_id=0, has_side_effects=True, vmem_limit_bytes=VMEM_BYTES - total * dim * 4 - SPARE),
    )(h_a, h_b, w1, w2, w3, *affine)


def emit_kernel(rows, grads, bn, loss, *refs):
    big, small, (sem,) = refs[:3], refs[3:8], refs[8:]
    copies = [pltpu.make_async_copy(grads.at[pl.ds(lo, hi - lo)], dst, sem.at[i]) for i, (dst, (lo, hi)) in enumerate(zip(big, rows))]
    for cp in copies:
        cp.start()
    for i in range(4):
        small[i][...] = bn[one(i), :]
    small[4][...] = loss[...]
    for cp in copies:
        cp.wait()


def emit(grads, bn, loss, dim):
    total = grads.shape[0]
    rows = ((2 * dim, total), (dim, 2 * dim), (0, dim))
    any_spec = pl.BlockSpec(memory_space=pl.ANY)
    vm = pl.BlockSpec(memory_space=pltpu.VMEM)
    vec = jax.ShapeDtypeStruct((1, dim), F32)
    return pl.pallas_call(
        functools.partial(emit_kernel, rows),
        name='emit',
        out_shape=[jax.ShapeDtypeStruct((hi - lo, dim), F32) for lo, hi in rows] + [vec] * 4 + [jax.ShapeDtypeStruct((1, LANES), F32)],
        in_specs=[vm, vm, vm],
        out_specs=[any_spec] * 3 + [vm] * 5,
        scratch_shapes=[pltpu.SemaphoreType.DMA((3,))],
        compiler_params=pltpu.CompilerParams(vmem_limit_bytes=VMEM_BYTES // 16),
    )(*(pltpu.with_memory_space_constraint(v, pltpu.VMEM) for v in (grads, bn, loss)))


def solution(mesh):
    n_dev = mesh.shape['data']

    def local_step(h_a, h_b, w_one, w_two, w_three, gain_one, bias_one, gain_two, bias_two):
        affine = [v.reshape(1, -1) for v in (gain_one, bias_one, gain_two, bias_two)]
        grads, bn, loss, _ = train_step(n_dev, h_a, h_b, w_one, w_two, w_three, *affine)
        d_one, d_two, d_three, *small, loss = emit(grads, bn, loss, w_two.shape[0])
        return (loss[0, 0], d_one, d_two, d_three) + tuple(v.reshape(-1) for v in small)

    row = P('data', None)
    return jax.shard_map(local_step, mesh=mesh, in_specs=(row, row) + (P(),) * 7, out_specs=(P(),) * 8, check_vma=False)
```

time: 233 us -> 228 us (0.979)
  Pallas kernels: 232 us -> 227 us
    pallas_call x2 -> x1, Pallas kernels: 226 us -> 221 us  [train_step(): pl.pallas_call(functools.partial(step_kernel, rows * n_dev), name='train_...]
where the time goes in v3:
time: 228 us
  Pallas kernels  227 us (100%)
    pallas_call x1, Pallas kernels, train_step(): pl.pallas_call(functools.partial(step_kernel, rows * n_dev), name='train_...  221 us
    pallas_call x1, Pallas kernels, emit(): pl.pallas_call(functools.partial(emit_kernel, rows), name='emit', out_sha...  6.67 us

profile of v3, /device:TPU:0, one launch (start us, length us, event | category | flops | bytes accessed | tf_op | source)
XLA Modules:
  0.0 228.2 jit_solution(18429827895522034535)
XLA Ops:
  0.6 220.7 %train_step.1 = (f32[4096,1024]{1,0:T(8,128)S(1)}, f32[4,1024]{1,0:T(4,128)S(1)}, f32[1,128]{1,0:T(1,128)S(1)}, f32[2048,1024]{1,0:T(8,128)}) custom-call(bf16[1024,2048]{1,0:T(8,128)(2,1)} %h_a.1, bf16[1024,2048]{1,0:T(8,128)(2,1)} %h_b.1, bf16[2048,1024]{1,0:T(8,128)(2,1)} %w1.1, bf16[1024,1024]{1,0:T(8,128)(2,1)} %w2.1, bf16[1024,1024]{1,0:T(8,128)(2,1)} %w3.1, ...), custom_call_target="tpu_custom_call" | custom-call | tf_op jit(solution)/shard_map/train_step/pallas_call | solution.py:618
  221.4 6.7 %emit.1 = (f32[2048,1024]{1,0:T(8,128)}, f32[1024,1024]{1,0:T(8,128)}, f32[1024,1024]{1,0:T(8,128)}, f32[1,1024]{1,0:T(1,128)}, f32[1,1024]{1,0:T(1,128)}, /*ind...) custom-call(f32[4096,1024]{1,0:T(8,128)S(1)} %get-tuple-element.19.grads, f32[4,1024]{1,0:T(4,128)S(1)} %get-tuple-element.20.bn, ...), custom_call_target="tpu_custom_call" | custom-call | tf_op jit(solution)/shard_map/emit/pallas_call | solution.py:656

commit v4 on v3

--- a/solution.py
+++ b/solution.py
@@ -83,11 +83,14 @@
         return self.flip(o & 4, o & 2, o & 1)
 
 
-def entry_barrier(place):
+def greet(place):
     barrier = pltpu.get_barrier_semaphore()
     for o in range(1, NDEV):
         pl.semaphore_signal(barrier, inc=1, device_id=(place.peer(o),), device_id_type=MESH)
-    pl.semaphore_wait(barrier, NDEV - 1)
+
+
+def meet():
+    pl.semaphore_wait(pltpu.get_barrier_semaphore(), NDEV - 1)
 
 
 class StatExchange:
@@ -234,7 +237,7 @@
 CHUNK, SMALL = 256, 128
 LEAD, EVEN, TAIL = 0, 16, 0
 COUNT = LEAD + EVEN + TAIL
-PART_SLOTS, CORE_SLOTS, LINK_SLOTS = 3, 2, 4
+PART_SLOTS, CORE_SLOTS, LINK_SLOTS = 3, 3, 4
 LAST_STEP = 6
 
 
@@ -278,8 +281,8 @@
         if k == LAST_STEP:
             red.drain_full()
 
-    def steps(self, t):
-        for k in range(1, LAST_STEP + 1):
+    def steps(self, t, first=1, last=LAST_STEP):
+        for k in range(first, last + 1):
             if not isinstance(t, int) or 0 <= t - k < COUNT:
                 self.step(k, t - k)
 
@@ -289,19 +292,22 @@
 
 def step_kernel(all_rows, h_a, h_b, w1, w2, w3, g1, b1, g2, b2,
                 grads, bn_o, loss_o, n1_o,
-                hbuf, w1b, w2b, w3b, x1, x2, nb, ghat, part, net, invs,
+                affine_b, hbuf, w1b, w2b, w3b, x1, x2, nb, ghat, part, net, invs,
                 st_src, st_rcv, zs_src, zs_rcv, ls_src, ls_rcv,
                 ld_sem, n_sem, h_sem, st_ss, st_rs, zs_ss, zs_rs, ls_ss, ls_rs, gr_ss, gr_rs, rd_ss, rd_rs):
     dim = w2b.shape[0]
     rows, feat = h_a.shape
-    affine = ((g1, b1), (g2, b2))
+    affine = ((affine_b.at[0], affine_b.at[1]), (affine_b.at[2], affine_b.at[3]))
     view = [slice(0, rows), slice(rows, 2 * rows)]
     low, high = slice(0, 2 * dim), slice(2 * dim, 2 * dim + feat)
     u1, dxb = grads.at[low], grads.at[high]
     place = Place()
+    greet(place)
     h_all = (h_a, h_b)
+    strip = lambda i: slice(i * ROWS, i * ROWS + ROWS)
     loads = {}
-    for name, src, dst in (('w1', w1, w1b), ('ha', h_a, hbuf.at[view[0]]), ('hb', h_b, hbuf.at[view[1]]), ('w2', w2, w2b), ('w3', w3, w3b)):
+    for name, src, dst in (('w1', w1, w1b), *(('ha%d' % i, h_a.at[strip(i)], hbuf.at[strip(i)]) for i in range(rows // ROWS)), ('hb', h_b, hbuf.at[view[1]]), ('w2', w2, w2b), ('w3', w3, w3b),
+                           *(('affine%d' % i, src, affine_b.at[i]) for i, src in enumerate((g1, b1, g2, b2)))):
         loads[name] = pltpu.make_async_copy(src, dst, ld_sem.at[len(loads)])
         loads[name].start()
     spill = [pltpu.make_async_copy(u1.at[view[v]], n1_o.at[view[v]], n_sem.at[v]) for v in (0, 1)]
@@ -310,7 +316,6 @@
     def lanes(row, size):
         return pl.ds(pl.multiple_of(row, SMALL), size)
 
-    entry_barrier(place)
     stats = StatExchange(place, st_src, st_rcv, st_ss, st_rs)
     zstats = StatExchange(place, zs_src, zs_rcv, zs_ss, zs_rs)
     lstats = StatExchange(place, ls_src, ls_rcv, ls_ss, ls_rs)
@@ -320,7 +325,17 @@
             dst[rws, :] = out
             return out, out * out
 
-        st_src[slot, ROW0, :], st_src[slot, ROW1, :] = by_rows(lhs, rhs, use, 2)
+        if slot:
+            sums = by_rows(lhs, rhs, use, 2)
+        else:
+            sums = None
+            for i in range(rows // ROWS):
+                loads['ha%d' % i].wait()
+                out = dot(lhs[strip(i), :], rhs[...])
+                terms = [col_sum(t) for t in use(strip(i), out)]
+                sums = [a + b for a, b in zip(sums, terms)] if i else terms
+            meet()
+        st_src[slot, ROW0, :], st_src[slot, ROW1, :] = sums
         stats.send(slot)
 
     def norm_relu(slot, v, layer, ubuf, xbuf):
@@ -492,12 +507,12 @@
         loop(rows // STRIP, body)
 
     loads['w1'].wait()
-    loads['ha'].wait()
     linear(0, u1.at[view[0]], hbuf.at[view[0]], w1b)
     loads['hb'].wait()
     linear(1, u1.at[view[1]], hbuf.at[view[1]], w1b)
-    loads['w2'].wait()
-    loads['w3'].wait()
+    for name in list(loads):
+        if name[0] not in 'h1' and name != 'w1':
+            loads[name].wait()
     for v in (0, 1):
         norm_relu(v, v, 0, u1, x1)
         spill[v].start()
@@ -516,28 +531,28 @@
     gram_of(1, 0)
     gram_of(1, 1)
     a0.step_2()
+    b0.step_1()
+    b1.step_1()
+    a1.step_2()
     ztot = zstats.total(0)
     mus = [ztot[one(v)] / all_rows for v in (0, 1)]
     sq_sum = jnp.sum(ztot[one(2)])
-    b0.step_1()
-    a1.step_2()
-    b1.step_1()
     for cp in spill:
         cp.wait()
     store_outer(mus)
     a0.step_3(finish(0, 0))
     a1.step_3(finish(0, 1))
+    b0.step_2()
     a0.step_4()
-    b0.step_2()
+    b1.step_2()
     a1.step_4()
-    b1.step_2()
     b0.step_3(finish(1, 0))
-    a0.step_5()
     b1.step_3(finish(1, 1))
     lstats.send(0)
+    b0.step_4()
+    a0.step_5()
+    b1.step_4()
     a1.step_5()
-    b0.step_4()
-    b1.step_4()
     a0.step_6()
     a1.step_6()
     expand(0)
@@ -573,7 +588,8 @@
         weight_grad(t, x2.at[:, lanes(lax.rem(t, 2) * CHUNK, chunk_of(t)[1])], du1)
 
     for t in range(first_one):
-        chunks.steps(t)
+        early = t < PART_SLOTS
+        chunks.steps(t, 1, t - 1 if early else LAST_STEP)
         if t == first_two:
             for v in (0, 1):
                 grad_pre(4 + v, v, 1, dub)
@@ -586,6 +602,8 @@
             weight_grad(t, x2.at[:, lanes(row, size)], dzb)
         else:
             weight_grad(t, x1.at[:, lanes(row - dim, size)], dub)
+        if early:
+            chunks.steps(t, max(t, 1))
         if t in extra:
             extra[t]()
 
@@ -619,30 +637,28 @@
         functools.partial(step_kernel, rows * n_dev),
         name='train_step',
         out_shape=[pltpu.VMEM((total, dim), F32), pltpu.VMEM((4, dim), F32), pltpu.VMEM((1, LANES), F32), jax.ShapeDtypeStruct(wide, F32)],
-        in_specs=[any_spec] * 5 + [vm] * 4,
+        in_specs=[any_spec] * 9,
         out_specs=[vm] * 3 + [any_spec],
         scratch_shapes=[
-            pltpu.VMEM((2 * rows, feat), BF16), pltpu.VMEM((feat, dim), BF16), pltpu.VMEM((dim, dim), BF16), pltpu.VMEM((dim, dim), BF16),
+            pltpu.VMEM((4, 1, dim), F32), pltpu.VMEM((2 * rows, feat), BF16), pltpu.VMEM((feat, dim), BF16), pltpu.VMEM((dim, dim), BF16), pltpu.VMEM((dim, dim), BF16),
             pltpu.VMEM(wide, BF16), pltpu.VMEM(wide, BF16), pltpu.VMEM(wide, F32), pltpu.VMEM((2, PACKED, BLK), BF16),
             pltpu.VMEM((PART_SLOTS * CHUNK, dim), F32), pltpu.VMEM((CORE_SLOTS * CHUNK // 2 + LINK_SLOTS * CHUNK * 3 // 8, dim), F32),
             pltpu.VMEM((4, dim), F32),
             pltpu.VMEM((8,) + moments, F32), pltpu.VMEM((8, NDEV) + moments, F32),
             pltpu.VMEM((1, 4, dim), F32), pltpu.VMEM((1, NDEV, 4, dim), F32),
             pltpu.VMEM((1, 1, LANES), F32), pltpu.VMEM((1, NDEV, 1, LANES), F32),
-            dma((5,)), dma((2,)), dma((2, 2)), dma((8, NDEV)), dma((8, NDEV)), dma((1, NDEV)), dma((1, NDEV)), dma((1, NDEV)), dma((1, NDEV)),
+            dma((8 + rows // ROWS,)), dma((2,)), dma((2, 2)), dma((8, NDEV)), dma((8, NDEV)), dma((1, NDEV)), dma((1, NDEV)), dma((1, NDEV)), dma((1, NDEV)),
             dma((2, 2, 10)), dma((2, 2, 10)), dma((COUNT, 10)), dma((COUNT, 10))],
         compiler_params=pltpu.CompilerParams(collective_id=0, has_side_effects=True, vmem_limit_bytes=VMEM_BYTES - total * dim * 4 - SPARE),
     )(h_a, h_b, w1, w2, w3, *affine)
 
 
 def emit_kernel(rows, grads, bn, loss, *refs):
-    big, small, (sem,) = refs[:3], refs[3:8], refs[8:]
-    copies = [pltpu.make_async_copy(grads.at[pl.ds(lo, hi - lo)], dst, sem.at[i]) for i, (dst, (lo, hi)) in enumerate(zip(big, rows))]
+    outs, sem = refs[:-1], refs[-1]
+    srcs = [grads.at[pl.ds(lo, hi - lo)] for lo, hi in rows] + [bn.at[one(i)] for i in range(4)] + [loss]
+    copies = [pltpu.make_async_copy(src, dst, sem.at[i]) for i, (src, dst) in enumerate(zip(srcs, outs))]
     for cp in copies:
         cp.start()
-    for i in range(4):
-        small[i][...] = bn[one(i), :]
-    small[4][...] = loss[...]
     for cp in copies:
         cp.wait()
 
@@ -658,8 +674,8 @@
         name='emit',
         out_shape=[jax.ShapeDtypeStruct((hi - lo, dim), F32) for lo, hi in rows] + [vec] * 4 + [jax.ShapeDtypeStruct((1, LANES), F32)],
         in_specs=[vm, vm, vm],
-        out_specs=[any_spec] * 3 + [vm] * 5,
-        scratch_shapes=[pltpu.SemaphoreType.DMA((3,))],
+        out_specs=[any_spec] * 8,
+        scratch_shapes=[pltpu.SemaphoreType.DMA((8,))],
         compiler_params=pltpu.CompilerParams(vmem_limit_bytes=VMEM_BYTES // 16),
     )(*(pltpu.with_memory_space_constraint(v, pltpu.VMEM) for v in (grads, bn, loss)))
 

time: 228 us -> 226 us (level)
  no operation moved by 1% of the time
where the time goes in v4:
time: 226 us
  Pallas kernels  225 us (100%)
    pallas_call x1, Pallas kernels, train_step(): pl.pallas_call(functools.partial(step_kernel, rows * n_dev), name='train_...  219 us
    pallas_call x1, Pallas kernels, emit(): pl.pallas_call(functools.partial(emit_kernel, rows), name='emit', out_sha...  6.12 us

profile of v4, /device:TPU:0, one launch (start us, length us, event | category | flops | bytes accessed | tf_op | source)
XLA Modules:
  0.0 225.9 jit_solution(15125999702363112587)
XLA Ops:
  0.6 219.0 %train_step.1 = (f32[4096,1024]{1,0:T(8,128)S(1)}, f32[4,1024]{1,0:T(4,128)S(1)}, f32[1,128]{1,0:T(1,128)S(1)}, f32[2048,1024]{1,0:T(8,128)}) custom-call(bf16[1024,2048]{1,0:T(8,128)(2,1)} %h_a.1, bf16[1024,2048]{1,0:T(8,128)(2,1)} %h_b.1, bf16[2048,1024]{1,0:T(8,128)(2,1)} %w1.1, bf16[1024,1024]{1,0:T(8,128)(2,1)} %w2.1, bf16[1024,1024]{1,0:T(8,128)(2,1)} %w3.1, ...), custom_call_target="tpu_custom_call" | custom-call | tf_op jit(solution)/shard_map/train_step/pallas_call | solution.py:636
  219.6 6.1 %emit.1 = (f32[2048,1024]{1,0:T(8,128)}, f32[1024,1024]{1,0:T(8,128)}, f32[1024,1024]{1,0:T(8,128)}, f32[1,1024]{1,0:T(1,128)}, f32[1,1024]{1,0:T(1,128)}, /*ind...) custom-call(f32[4096,1024]{1,0:T(8,128)S(1)} %get-tuple-element.19.grads, f32[4,1024]{1,0:T(4,128)S(1)} %get-tuple-element.20.bn, ...), custom_call_target="tpu_custom_call" | custom-call | tf_op jit(solution)/shard_map/emit/pallas_call | solution.py:672

commit v5 on v4

--- a/solution.py
+++ b/solution.py
@@ -15,6 +15,7 @@
 NDEV = 8
 BLK = 256
 STRIP = 64
+SETS = 4
 SPARE = 524288
 ROWS = 512
 VMEM_BYTES = 67043328
@@ -102,7 +103,7 @@
         place = self.place
         return [pltpu.make_async_remote_copy(
             src_ref=self.src.at[slot], dst_ref=self.rcv.at[slot, place.me],
-            send_sem=self.ssem.at[slot, o], recv_sem=self.rsem.at[slot, o],
+            send_sem=self.ssem.at[slot % SETS, o], recv_sem=self.rsem.at[slot % SETS, o],
             device_id=(place.peer(o),), device_id_type=MESH) for o in range(1, NDEV)]
 
     def send(self, slot):
@@ -123,6 +124,7 @@
         for slot in self.sent:
             for cp in self.copies(slot):
                 cp.wait_send()
+        self.sent = []
 
 
 class Reduce:
@@ -266,7 +268,7 @@
         return Reduce(self.place, self.part_of(t), self.out.at[pl.ds(pl.multiple_of(row, SMALL), size)],
                       landing(0, lax.rem(t, CORE_SLOTS), CHUNK // 2, size // 2),
                       [landing(one_base, 2 * link + k, CHUNK // 8, size // 8) for k in (0, 1)],
-                      [landing(two_base, 2 * link + k, CHUNK // 16, size // 16) for k in (0, 1)], self.ssem.at[t], self.rsem.at[t])
+                      [landing(two_base, 2 * link + k, CHUNK // 16, size // 16) for k in (0, 1)], self.ssem.at[lax.rem(t, SETS)], self.rsem.at[lax.rem(t, SETS)])
 
     def part_of(self, t):
         return self.part.at[pl.ds(pl.multiple_of(lax.rem(t, PART_SLOTS) * CHUNK, CHUNK), chunk_of(t)[1])]
@@ -294,7 +296,7 @@
                 grads, bn_o, loss_o, n1_o,
                 affine_b, hbuf, w1b, w2b, w3b, x1, x2, nb, ghat, part, net, invs,
                 st_src, st_rcv, zs_src, zs_rcv, ls_src, ls_rcv,
-                ld_sem, n_sem, h_sem, st_ss, st_rs, zs_ss, zs_rs, ls_ss, ls_rs, gr_ss, gr_rs, rd_ss, rd_rs):
+                ld_sem, n_sem, h_sem, st_ss, st_rs, ls_ss, ls_rs, rd_ss, rd_rs):
     dim = w2b.shape[0]
     rows, feat = h_a.shape
     affine = ((affine_b.at[0], affine_b.at[1]), (affine_b.at[2], affine_b.at[3]))
@@ -317,7 +319,7 @@
         return pl.ds(pl.multiple_of(row, SMALL), size)
 
     stats = StatExchange(place, st_src, st_rcv, st_ss, st_rs)
-    zstats = StatExchange(place, zs_src, zs_rcv, zs_ss, zs_rs)
+    zstats = StatExchange(place, zs_src, zs_rcv, st_ss, st_rs)
     lstats = StatExchange(place, ls_src, ls_rcv, ls_ss, ls_rs)
 
     def linear(slot, dst, lhs, rhs):
@@ -404,7 +406,7 @@
             r1 = [net.at[pl.ds(k * n // 8, n // 8), bd] for k in (0, 1)]
             r2 = [net.at[pl.ds(n // 4 + k * n // 16, n // 16), bd] for k in (0, 1)]
             pair.append(GramReduce(place, gram.at[pl.ds(0, n), bd], ghat.at[v, pl.ds(lo, n)], part.at[pl.ds(0, n // 2), bd], r1, r2,
-                                   gr_ss.at[v, ch], gr_rs.at[v, ch]))
+                                   rd_ss.at[2 * v + ch], rd_rs.at[2 * v + ch]))
         reds.append(pair)
     (a0, a1), (b0, b1) = reds
 
@@ -527,6 +529,7 @@
     a0.step_1()
     a1.step_1()
     project(1)
+    stats.drain()
     zstats.send(0)
     gram_of(1, 0)
     gram_of(1, 1)
@@ -564,8 +567,10 @@
     b1.step_6()
     expand(1)
     grad_z(1, mus[1], [])
+    zstats.drain()
     for red in (a0, a1, b0, b1):
         red.drain_part()
+        red.drain_full()
 
     dub, du1 = w1b, hbuf.at[:, zcol]
     first_two = next(t for t in range(COUNT) if chunk_of(t)[0] >= dim)
@@ -618,10 +623,8 @@
         if t < COUNT:
             weight_tick(t)
     loss_o[...] = jnp.broadcast_to(jnp.sum(lstats.total(0)) + 2.0 * sq_sum / all_rows, loss_o.shape)
-    for ex in (stats, zstats, lstats):
-        ex.drain()
-    for red in (a0, a1, b0, b1):
-        red.drain_full()
+    stats.drain()
+    lstats.drain()
 
 
 def train_step(n_dev, h_a, h_b, w1, w2, w3, *affine):
@@ -647,8 +650,8 @@
             pltpu.VMEM((8,) + moments, F32), pltpu.VMEM((8, NDEV) + moments, F32),
             pltpu.VMEM((1, 4, dim), F32), pltpu.VMEM((1, NDEV, 4, dim), F32),
             pltpu.VMEM((1, 1, LANES), F32), pltpu.VMEM((1, NDEV, 1, LANES), F32),
-            dma((8 + rows // ROWS,)), dma((2,)), dma((2, 2)), dma((8, NDEV)), dma((8, NDEV)), dma((1, NDEV)), dma((1, NDEV)), dma((1, NDEV)), dma((1, NDEV)),
-            dma((2, 2, 10)), dma((2, 2, 10)), dma((COUNT, 10)), dma((COUNT, 10))],
+            dma((8 + rows // ROWS,)), dma((2,)), dma((2, 2)), dma((SETS, NDEV)), dma((SETS, NDEV)), dma((1, NDEV)), dma((1, NDEV)),
+            dma((SETS, 10)), dma((SETS, 10))],
         compiler_params=pltpu.CompilerParams(collective_id=0, has_side_effects=True, vmem_limit_bytes=VMEM_BYTES - total * dim * 4 - SPARE),
     )(h_a, h_b, w1, w2, w3, *affine)
 

time: 226 us -> 223 us (0.987)
  Pallas kernels: 225 us -> 222 us
    pallas_call x1, Pallas kernels: 219 us -> 216 us  [train_step(): pl.pallas_call(functools.partial(step_kernel, rows * n_dev), name='train_...]
where the time goes in v5:
time: 223 us
  Pallas kernels  222 us (100%)
    pallas_call x1, Pallas kernels, train_step(): pl.pallas_call(functools.partial(step_kernel, rows * n_dev), name='train_...  216 us
    pallas_call x1, Pallas kernels, emit(): pl.pallas_call(functools.partial(emit_kernel, rows), name='emit', out_sha...  6.12 us

profile of v5, /device:TPU:0, one launch (start us, length us, event | category | flops | bytes accessed | tf_op | source)
XLA Modules:
  0.0 222.7 jit_solution(13327116800931040028)
XLA Ops:
  0.6 215.7 %train_step.1 = (f32[4096,1024]{1,0:T(8,128)S(1)}, f32[4,1024]{1,0:T(4,128)S(1)}, f32[1,128]{1,0:T(1,128)S(1)}, f32[2048,1024]{1,0:T(8,128)}) custom-call(bf16[1024,2048]{1,0:T(8,128)(2,1)} %h_a.1, bf16[1024,2048]{1,0:T(8,128)(2,1)} %h_b.1, bf16[2048,1024]{1,0:T(8,128)(2,1)} %w1.1, bf16[1024,1024]{1,0:T(8,128)(2,1)} %w2.1, bf16[1024,1024]{1,0:T(8,128)(2,1)} %w3.1, ...), custom_call_target="tpu_custom_call" | custom-call | tf_op jit(solution)/shard_map/train_step/pallas_call | solution.py:639
  216.4 6.1 %emit.1 = (f32[2048,1024]{1,0:T(8,128)}, f32[1024,1024]{1,0:T(8,128)}, f32[1024,1024]{1,0:T(8,128)}, f32[1,1024]{1,0:T(1,128)}, f32[1,1024]{1,0:T(1,128)}, /*ind...) custom-call(f32[4096,1024]{1,0:T(8,128)S(1)} %get-tuple-element.19.grads, f32[4,1024]{1,0:T(4,128)S(1)} %get-tuple-element.20.bn, ...), custom_call_target="tpu_custom_call" | custom-call | tf_op jit(solution)/shard_map/emit/pallas_call | solution.py:675

commit v6 on v5

--- a/solution.py
+++ b/solution.py
@@ -433,8 +433,10 @@
             return jnp.where(eye, -on / (2.0 * std), 4.0 * cov).astype(BF16)
         return fin
 
-    def expand(v):
+    def expand(v, ch):
         for row, lane, r, c, size, mirrored in PIECES:
+            if int(row >= SPLIT) != ch:
+                continue
             blk = ghat[v, row:row + size, lane:lane + size]
             w1b[v * dim + r:v * dim + r + size, c:c + size] = blk
             if mirrored:
@@ -557,15 +559,17 @@
     b1.step_4()
     a1.step_5()
     a0.step_6()
+    expand(0, 0)
     a1.step_6()
-    expand(0)
+    expand(0, 1)
     grad_z(0, mus[0], [b0.step_5])
     lead = lanes(0, chunk_of(0)[1])
     chunks.part_of(0)[...] = dot(x2[view[0], lead], dzb[view[0], :], TN)
     b1.step_5()
     b0.step_6()
+    expand(1, 0)
     b1.step_6()
-    expand(1)
+    expand(1, 1)
     grad_z(1, mus[1], [])
     zstats.drain()
     for red in (a0, a1, b0, b1):
@@ -616,15 +620,15 @@
         chunks.steps(t)
         weight_tick(t)
 
+    loss_o[...] = jnp.broadcast_to(jnp.sum(lstats.total(0)) + 2.0 * sq_sum / all_rows, loss_o.shape)
+    stats.drain()
+    lstats.drain()
     last_even = LEAD + EVEN - 1
     loop(last_even - first_one, lambda i: tick(first_one + i))
     for t in range(last_even, COUNT + LAST_STEP):
         chunks.steps(t)
         if t < COUNT:
             weight_tick(t)
-    loss_o[...] = jnp.broadcast_to(jnp.sum(lstats.total(0)) + 2.0 * sq_sum / all_rows, loss_o.shape)
-    stats.drain()
-    lstats.drain()
 
 
 def train_step(n_dev, h_a, h_b, w1, w2, w3, *affine):

time: 223 us -> 222 us (level)
  no operation moved by 1% of the time
where the time goes in v6:
time: 222 us
  Pallas kernels  221 us (100%)
    pallas_call x1, Pallas kernels, train_step(): pl.pallas_call(functools.partial(step_kernel, rows * n_dev), name='train_...  215 us
    pallas_call x1, Pallas kernels, emit(): pl.pallas_call(functools.partial(emit_kernel, rows), name='emit', out_sha...  6.12 us

profile of v6, /device:TPU:0, one launch (start us, length us, event | category | flops | bytes accessed | tf_op | source)
XLA Modules:
  0.0 222.2 jit_solution(1258818147148621170)
XLA Ops:
  0.6 215.2 %train_step.1 = (f32[4096,1024]{1,0:T(8,128)S(1)}, f32[4,1024]{1,0:T(4,128)S(1)}, f32[1,128]{1,0:T(1,128)S(1)}, f32[2048,1024]{1,0:T(8,128)}) custom-call(bf16[1024,2048]{1,0:T(8,128)(2,1)} %h_a.1, bf16[1024,2048]{1,0:T(8,128)(2,1)} %h_b.1, bf16[2048,1024]{1,0:T(8,128)(2,1)} %w1.1, bf16[1024,1024]{1,0:T(8,128)(2,1)} %w2.1, bf16[1024,1024]{1,0:T(8,128)(2,1)} %w3.1, ...), custom_call_target="tpu_custom_call" | custom-call | tf_op jit(solution)/shard_map/train_step/pallas_call | solution.py:643
  215.9 6.1 %emit.1 = (f32[2048,1024]{1,0:T(8,128)}, f32[1024,1024]{1,0:T(8,128)}, f32[1024,1024]{1,0:T(8,128)}, f32[1,1024]{1,0:T(1,128)}, f32[1,1024]{1,0:T(1,128)}, /*ind...) custom-call(f32[4096,1024]{1,0:T(8,128)S(1)} %get-tuple-element.19.grads, f32[4,1024]{1,0:T(4,128)S(1)} %get-tuple-element.20.bn, ...), custom_call_target="tpu_custom_call" | custom-call | tf_op jit(solution)/shard_map/emit/pallas_call | solution.py:679
